TPU v7x, 256 devices: a whole 4x4x8 slice. The times are simulated.
256 devices in a mesh: grp: 4 (over x), gx: 16 (over z, core), gy: 4 (over y).
Axes of the slice: x: 4, y: 4, z: 8, core: 2. Of those that a mesh axis runs over, the one named last changes fastest.
Arguments:
- conserved: float32 [8, 4, 128, 64, 128], P(None, 'grp', 'gx', 'gy'), may hold values from -6 to 6
- velocity: float32 [3, 4, 128, 64, 128], P(None, 'grp', 'gx', 'gy'), may hold values from -0.45 to 0.45
- donor_corner: int32 [4, 16, 4, 4, 64, 32], P('grp', 'gx', 'gy'), may hold values from 0 to 14206, as said below
- donor_fraction: float32 [3, 4, 16, 4, 4, 64, 32], P(None, 'grp', 'gx', 'gy'), may hold values from 0 to 1
- target_cell: int32 [4, 16, 4, 4, 64, 32], P('grp', 'gx', 'gy'), may hold values from 0 to 16384, as said below
Outputs:
- advanced: float32 [8, 4, 128, 64, 128], P(None, 'grp', 'gx', 'gy')
Inputs may be any that keep to these rules, and one draw needn't show every extreme that they name: `donor_corner`: each used slot's stencil lies inside the donor device's block (x < 7, y < 15, z < 127); entries of empty slots are 0. Slot s of a pair is used exactly when s is below that pair's count, the same count as in target_cell; a pair's count is at most 32; every device fills 32 slots on the device of the same index in the grid two further on (grid indices modulo 4); devices of one grid fill none on each other, and the two background halves (grids 2 and 3) fill none on each other. `target_cell`: used slots match donor_corner's used slots; on one receiving device the named cells are distinct and lie within 32 layers of either end of the third dimension; empty slots hold 16384.
All inputs are finite; a program needn't handle non-finite values.
Results may differ from a plain program's by a relative error of at most 0.00002.
Values sent between devices are 32-bit elements; how exact they have to be, the bound alone decides.
A program may use at most 128 MiB of HBM per device.

v0:
```python
import jax
import jax.numpy as jnp
from jax import lax
from jax.sharding import PartitionSpec as P

signal_speed = 0.5
courant_number = 0.3
corner_shifts = (
    (0, 0, 0),
    (0, 0, 1),
    (0, 1, 0),
    (0, 1, 1),
    (1, 0, 0),
    (1, 0, 1),
    (1, 1, 0),
    (1, 1, 1),
)


def in_blocks(array, dim, devices):
    before, after = (array.shape[:dim], array.shape[dim + 1 :])
    return jnp.moveaxis(array.reshape(*before, devices, -1, *after), dim, 0)


def in_order(blocks, dim):
    blocks = jnp.moveaxis(blocks, 0, dim)
    lengths = blocks.shape
    return blocks.reshape(*lengths[:dim], lengths[dim] * lengths[dim + 1], *lengths[dim + 2 :])


def joined_exchange(array, axis, axes, splits, concats):
    sizes = [lax.axis_size(a) for a in axes]
    blocks = in_blocks(array, splits[0], sizes[0])
    blocks = jnp.moveaxis(in_blocks(blocks, splits[1] + 1, sizes[1]), 0, 1)
    inside = blocks.shape[2:]
    blocks = blocks.reshape(-1, *inside)
    blocks = lax.all_to_all(blocks, axis, split_axis=0, concat_axis=0, tiled=True)
    blocks = in_order(blocks.reshape(*sizes, *inside), concats[0] + 1)
    return in_order(blocks, concats[1])


def extended(array, sides, width):
    edges = {}
    for axis, dim in sides:
        devices, length = (lax.axis_size(axis), array.shape[dim])
        up = [(i, (i + 1) % devices) for i in range(devices - 1)]
        last = lax.slice_in_dim(array, length - width, length, axis=dim)
        leading = lax.slice_in_dim(array, 0, width, axis=dim)
        edges[dim] = (
            lax.ppermute(last, axis, up),
            lax.ppermute(leading, axis, [(b, a) for a, b in up]),
        )
    done = []
    for _, dim in sides:
        low, high = edges[dim]
        around = [(width, width) if d in done else (0, 0) for d in range(array.ndim)]
        array = jnp.concatenate([jnp.pad(low, around), array, jnp.pad(high, around)], axis=dim)
        done.append(dim)
    return array


def gather_corners(flat_state, corner_base, stride_x, stride_y):
    pieces = [
        jnp.take(
            flat_state, corner_base + shift[0] * stride_x + shift[1] * stride_y + shift[2], axis=1
        )
        for shift in corner_shifts
    ]
    return jnp.stack(pieces)


def blend_corners(corners, fraction):
    total = jnp.zeros(corners.shape[1:], jnp.float32)
    for number, shift in enumerate(corner_shifts):
        weight_x = fraction[0] if shift[0] else 1.0 - fraction[0]
        weight_y = fraction[1] if shift[1] else 1.0 - fraction[1]
        weight_z = fraction[2] if shift[2] else 1.0 - fraction[2]
        weight = weight_x * weight_y * weight_z
        total = total + weight[None] * corners[number]
    return total


def face_pair(array, direction):
    low_index = [slice(None)] + [slice(1, -1)] * 3
    high_index = [slice(None)] + [slice(1, -1)] * 3
    low_index[direction] = slice(0, -1)
    high_index[direction] = slice(1, None)
    return (array[tuple(low_index)], array[tuple(high_index)])


def step_diff(array, direction):
    lower = [slice(None)] * 4
    upper = [slice(None)] * 4
    lower[direction] = slice(0, -1)
    upper[direction] = slice(1, None)
    return array[tuple(upper)] - array[tuple(lower)]


def central(field, direction):
    lower = [slice(1, -1)] * 3
    upper = [slice(1, -1)] * 3
    lower[direction] = slice(0, -2)
    upper[direction] = slice(2, None)
    return 0.5 * (field[tuple(upper)] - field[tuple(lower)])


def hll_flux(state_low, state_high, speed_low, speed_high):
    wave_low = jnp.minimum(jnp.minimum(speed_low, speed_high) - signal_speed, 0.0)
    wave_high = jnp.maximum(jnp.maximum(speed_low, speed_high) + signal_speed, 0.0)
    return (
        wave_high * speed_low * state_low
        - wave_low * speed_high * state_high
        + wave_low * wave_high * (state_high - state_low)
    ) / (wave_high - wave_low)


def advance(conserved, speeds):
    hydro = conserved[:5]
    magnetic = conserved[5:]
    change = jnp.zeros(hydro[:, 1:-1, 1:-1, 1:-1].shape, jnp.float32)
    for direction in (1, 2, 3):
        state_low, state_high = face_pair(hydro, direction)
        speed_low, speed_high = face_pair(speeds[direction - 1 : direction], direction)
        flux = hll_flux(state_low, state_high, speed_low, speed_high)
        change = change + step_diff(flux, direction)
    hydro_next = hydro[:, 1:-1, 1:-1, 1:-1] - courant_number * change
    elec_x = -(speeds[1] * magnetic[2] - speeds[2] * magnetic[1])
    elec_y = -(speeds[2] * magnetic[0] - speeds[0] * magnetic[2])
    elec_z = -(speeds[0] * magnetic[1] - speeds[1] * magnetic[0])
    curl_x = central(elec_z, 1) - central(elec_y, 2)
    curl_y = central(elec_x, 2) - central(elec_z, 0)
    curl_z = central(elec_y, 0) - central(elec_x, 1)
    magnetic_next = magnetic[:, 1:-1, 1:-1, 1:-1] - courant_number * jnp.stack(
        [curl_x, curl_y, curl_z]
    )
    return jnp.concatenate([hydro_next, magnetic_next], axis=0)


def per_device(conserved, velocity, donor_corner, donor_fraction, target_cell):
    var_count = conserved.shape[0]
    rows_x = conserved.shape[2]
    rows_y = conserved.shape[3]
    depth = conserved.shape[4]
    flat_state = conserved[:, 0].reshape(var_count, rows_x * rows_y * depth)
    corner_base = donor_corner[0, 0, 0]
    fraction = donor_fraction[:, 0, 0, 0]
    blended = blend_corners(
        gather_corners(flat_state, corner_base, rows_y * depth, depth), fraction
    )
    received = joined_exchange(blended, ("grp", "gx", "gy"), ("grp", ("gx", "gy")), (1, 2), (1, 2))
    targets = target_cell[0, 0, 0].reshape(-1)
    filled = flat_state.at[:, targets].set(received.reshape(var_count, -1), mode="drop")
    filled = filled.reshape(var_count, rows_x, rows_y, depth)
    stacked = jnp.concatenate([filled, velocity[:, 0]], axis=0)
    bordered = extended(stacked, (("gx", 1), ("gy", 2)), 1)
    bordered = jnp.pad(bordered, ((0, 0), (0, 0), (0, 0), (1, 1)))
    result = advance(bordered[:var_count], bordered[var_count:])
    return result[:, None]


def solution(mesh):
    return jax.shard_map(
        per_device,
        mesh=mesh,
        in_specs=(
            P(None, "grp", "gx", "gy", None),
            P(None, "grp", "gx", "gy", None),
            P("grp", "gx", "gy", None, None, None),
            P(None, "grp", "gx", "gy", None, None, None),
            P("grp", "gx", "gy", None, None, None),
        ),
        out_specs=P(None, "grp", "gx", "gy", None),
        check_vma=False,
    )
```

profile of v0, /device:TPU:1, one launch (start us, length us, event | category | flops | bytes accessed | tf_op | source)
XLA Modules:
  0.0 388.7 jit_solution(12213411973077418842)
XLA Ops:
  0.0 0.9 compare_select_fusion.8
  0.9 1.0 compare_and_fusion.7
  1.9 0.9 fusion.30
  2.9 0.9 bitcast_multiply_fusion.11
  3.8 5.9 %copy.55 = f32[8,1,8,16,128]{0,4,3,2,1:T(8,128)} copy(f32[8,1,8,16,128]{4,3,2,1,0:T(8,128)} %param.7) | data formatting | bytes 1048576 | tf_op args[0]
  9.7 0.1 copy.65
  9.9 0.1 copy.68
  10.1 31.2 %gather_fusion.2 = f32[8192,8]{1,0:T(8,128)} fusion(f32[8,16384]{0,1:T(8,128)} %bitcast.230, s32[8192]{0:T(1024)S(1)} %broadcast_clamp_fusion.5), kind=kCustom, calls=%fused_computation.2.clone | custom fusion | bytes 557056 | tf_op jit(solution)/shard_map/jit(_take)/gather | solution.py:64
  41.3 31.3 %gather_fusion.3 = f32[8192,8]{1,0:T(8,128)} fusion(f32[8,16384]{0,1:T(8,128)} %bitcast.231, s32[8192]{0:T(1024)S(1)} %broadcast_clamp_fusion.4), kind=kCustom, calls=%fused_computation.3.clone | custom fusion | bytes 557056 | tf_op jit(solution)/shard_map/jit(_take)/gather | solution.py:64
  72.6 0.1 copy.71
  72.8 31.3 %gather_fusion.4 = f32[8192,8]{1,0:T(8,128)} fusion(f32[8,16384]{0,1:T(8,128)} %bitcast.232, s32[8192]{0:T(1024)S(1)} %broadcast_clamp_fusion.3), kind=kCustom, calls=%fused_computation.4.clone | custom fusion | bytes 557056 | tf_op jit(solution)/shard_map/jit(_take)/gather | solution.py:64
  104.1 0.1 copy.74
  104.3 31.2 %gather_fusion.5 = f32[8192,8]{1,0:T(8,128)} fusion(f32[8,16384]{0,1:T(8,128)} %bitcast.233, s32[8192]{0:T(1024)S(1)} %broadcast_clamp_fusion.2), kind=kCustom, calls=%fused_computation.5.clone | custom fusion | bytes 557056 | tf_op jit(solution)/shard_map/jit(_take)/gather | solution.py:64
  135.7 31.3 %gather_fusion.6 = f32[8192,8]{1,0:T(8,128)} fusion(f32[8,16384]{0,1:T(8,128)} %bitcast.234, s32[8192]{0:T(1024)S(1)} %broadcast_clamp_fusion.1), kind=kCustom, calls=%fused_computation.6.clone | custom fusion | bytes 557056 | tf_op jit(solution)/shard_map/jit(_take)/gather | solution.py:64
  167.0 0.1 copy.80
  167.2 31.3 %gather_fusion.7 = f32[8192,8]{1,0:T(8,128)} fusion(f32[8,16384]{0,1:T(8,128)} %bitcast.235, s32[8192]{0:T(1024)S(1)} %broadcast_clamp_fusion), kind=kCustom, calls=%fused_computation.7.clone | custom fusion | bytes 557056 | tf_op jit(solution)/shard_map/jit(_take)/gather | solution.py:64
  198.7 31.3 %gather_fusion = f32[8192,8]{1,0:T(8,128)} fusion(f32[8,16384]{0,1:T(8,128)} %bitcast.236, s32[8192]{0:T(1024)S(1)} %broadcast_clamp_fusion.7), kind=kCustom, calls=%fused_computation.clone | custom fusion | bytes 557056 | tf_op jit(solution)/shard_map/jit(_take)/gather | solution.py:64
  229.9 0.1 copy.62
  230.1 31.2 %gather_fusion.1 = f32[8192,8]{1,0:T(8,128)} fusion(f32[8,16384]{0,1:T(8,128)} %bitcast.237, s32[8192]{0:T(1024)S(1)} %broadcast_clamp_fusion.6), kind=kCustom, calls=%fused_computation.1.clone | custom fusion | bytes 557056 | tf_op jit(solution)/shard_map/jit(_take)/gather | solution.py:64
  261.3 0.1 copy.58
  261.4 0.1 copy.61
  261.6 0.1 copy.64
  261.7 0.1 copy.67
  261.8 0.1 copy.70
  262.0 0.1 copy.73
  262.1 0.1 copy.76
  262.2 0.1 copy.79
  262.3 0.1 copy.57
  262.4 0.1 copy.63
  262.5 0.1 copy.66
  262.6 0.1 copy.69
  262.7 0.1 copy.72
  262.8 0.1 copy.75
  263.0 0.1 copy.60
  263.1 0.1 copy.78
  263.2 23.1 %fusion.1 = f32[4,64,8,1,1,32]{2,5,1,0,4,3:T(8,128)} fusion(f32[4,64,32,8]{3,2,1,0:T(8,128)} %bitcast.254, f32[4,64,32,8]{3,2,1,0:T(8,128)} %bitcast.253, f32[4,64,32,8]{3,2,1,0:T(8,128)} %bitcast.252, f32[4,64,32,8]{3,2,1,0:T(8,128)} %bitcast.251, f32[4,64,32,8]{3,2,1,0:T(8,128)} %bitcast.250, f32[4,64,32,8]{3,2,1,0:T(8,128)} %bitcast.249, ...), kind=kLoop, calls=%fused_computation.11 | loop fusion | flops 1507328 | bytes 2686976 | tf_op jit(solution)/shard_map/transpose;transpose | solution.py:34
  286.3 2.8 copy.81
  289.2 1.2 reshape.295
  290.3 15.6 %all-to-all-start = ((f32[256,1,256]{2,1,0:T(1,128)}), f32[256,1,256]{2,1,0:T(1,128)S(1)}, u32[]{:S(2)}, u32[]{:S(2)}) async-start(f32[256,1,256]{2,1,0:T(1,128)} %reshape.295), calls=%async_computation | async-start | bytes 524288 | tf_op jit(solution)/shard_map/all_to_all | solution.py:37
  306.0 0.1 copy.56
  306.1 0.1 reshape_squeeze.7
  306.3 15.4 %all-to-all-done = f32[256,1,256]{2,1,0:T(1,128)S(1)} async-done(((f32[256,1,256]{2,1,0:T(1,128)}), f32[256,1,256]{2,1,0:T(1,128)S(1)}, u32[]{:S(2)}, u32[]{:S(2)}) %all-to-all-start) | async-done | bytes 262176 | tf_op jit(solution)/shard_map/all_to_all | solution.py:37
  321.7 0.5 broadcast.367
  322.2 1.3 reduce
  323.5 0.3 reshape.296
  323.7 2.7 copy.82
  326.4 27.4 %scatter_fusion = f32[8,16384]{0,1:T(8,128)} fusion(f32[8,16384]{0,1:T(8,128)} %bitcast.238, s32[8192]{0:T(1024)S(1)} %bitcast.260, f32[8192,8]{1,0:T(8,128)} %bitcast.257), kind=kCustom, calls=%fused_computation.8 | custom fusion | bytes 819200 | tf_op jit(solution)/shard_map/scatter | solution.py:152
  353.8 5.2 %copy.83 = f32[8,8,16,128]{3,2,1,0:T(8,128)S(1)} copy(f32[8,8,16,128]{0,3,2,1:T(8,128)} %bitcast.239) | data formatting | bytes 1048576 | tf_op jit(solution)/shard_map/reshape | solution.py:153
  359.0 3.1 collective-permute-start
  362.2 1.9 collective-permute-start.1
  364.2 2.3 collective-permute-start.2
  366.4 1.5 collective-permute-start.3
  367.9 6.6 %slice.302 = f32[3,16384]{0,1:T(8,128)} slice(f32[8,16384]{0,1:T(8,128)} %scatter_fusion), slice={[5:8], [0:16384]} | slice | bytes 393216 | tf_op jit(solution)/shard_map/slice | solution.py:133
  374.5 5.2 %copy.84 = f32[5,8,16,128]{3,2,1,0:T(8,128)S(1)} copy(f32[5,8,16,128]{0,3,2,1:T(8,128)} %bitcast.240) | data formatting | bytes 655360 | tf_op jit(solution)/shard_map/slice | solution.py:126
  379.7 5.2 %copy.85 = f32[3,8,16,128]{3,2,1,0:T(8,128)S(1)} copy(f32[3,8,16,128]{0,3,2,1:T(8,128)} %bitcast.241) | data formatting | bytes 393216 | tf_op jit(solution)/shard_map/slice | solution.py:133
  385.1 1.2 select_maximum_fusion
  386.4 0.1 multiply_bitcast_fusion.2
  386.5 0.1 negate_bitcast_fusion.2
  386.8 0.2 fusion.24
  387.0 0.3 add_divide_fusion
  387.3 0.1 add_divide_fusion.2
  387.4 0.2 add_divide_fusion.1
  387.6 0.2 fusion.11
  387.9 0.8 maximum_bitcast_fusion
  (36 shorter events, 1.3 us)
Async XLA Ops:
  286.3 19.7 %copy-start.1 = (s32[1,1,1,4,64,32]{4,5,3,2,1,0:T(8,128)S(1)}, s32[1,1,1,4,64,32]{4,5,3,2,1,0:T(8,128)}, u32[]{:S(2)}) copy-start(s32[1,1,1,4,64,32]{4,5,3,2,1,0:T(8,128)} %param.11) | copy-start | bytes 98308
  290.3 31.4 %all-to-all-start = ((f32[256,1,256]{2,1,0:T(1,128)}), f32[256,1,256]{2,1,0:T(1,128)S(1)}, u32[]{:S(2)}, u32[]{:S(2)}) async-start(f32[256,1,256]{2,1,0:T(1,128)} %reshape.295), calls=%async_computation | async-start | bytes 524288 | tf_op jit(solution)/shard_map/all_to_all | solution.py:37
  353.8 5.2 %copy-start = (f32[3,1,8,16,128]{4,3,2,1,0:T(8,128)S(1)}, f32[3,1,8,16,128]{4,3,2,1,0:T(8,128)}, u32[]{:S(2)}) copy-start(f32[3,1,8,16,128]{4,3,2,1,0:T(8,128)} %param.8) | copy-start | bytes 589828
  359.0 26.0 %collective-permute-start = (f32[11,1,16,128]{3,2,1,0:T(8,128)S(1)}, f32[11,1,16,128]{3,2,1,0:T(8,128)S(1)}, u32[]{:S(2)}, u32[]{:S(2)}) collective-permute-start(f32[11,1,16,128]{3,2,1,0:T(8,128)S(1)} %get-tuple-element.19), channel_id=1, source_target_pairs={{0,4},{4,8},{8,12},{12,16},{16,20},{20,24},{24,28},{28,32},{32,36}... | collective-permute-start | bytes 270344 | tf_op jit(solution)/shard_map/ppermute | solution.py:50
  362.2 22.9 %collective-permute-start.1 = (f32[11,1,16,128]{3,2,1,0:T(8,128)S(1)}, f32[11,1,16,128]{3,2,1,0:T(8,128)S(1)}, u32[]{:S(2)}, u32[]{:S(2)}) collective-permute-start(f32[11,1,16,128]{3,2,1,0:T(8,128)S(1)} %get-tuple-element.20), channel_id=1, source_target_pairs={{4,0},{8,4},{12,8},{16,12},{20,16},{24,20},{28,24},{32,28},{36,32}... | collective-permute-start | bytes 270344 | tf_op jit(solution)/shard_map/ppermute | solution.py:51
  364.2 20.8 %collective-permute-start.2 = (f32[11,8,1,128]{3,2,1,0:T(1,128)S(1)}, f32[11,8,1,128]{3,2,1,0:T(1,128)S(1)}, u32[]{:S(2)}, u32[]{:S(2)}) collective-permute-start(f32[11,8,1,128]{3,2,1,0:T(1,128)S(1)} %get-tuple-element.21), channel_id=1, source_target_pairs={{0,1},{1,2},{2,3},{4,5},{5,6},{6,7},{8,9},{9,10},{10,11},{12,13},{... | collective-permute-start | bytes 135176 | tf_op jit(solution)/shard_map/ppermute | solution.py:50
  366.4 18.6 %collective-permute-start.3 = (f32[11,8,1,128]{3,2,1,0:T(1,128)S(1)}, f32[11,8,1,128]{3,2,1,0:T(1,128)S(1)}, u32[]{:S(2)}, u32[]{:S(2)}) collective-permute-start(f32[11,8,1,128]{3,2,1,0:T(1,128)S(1)} %get-tuple-element.22), channel_id=1, source_target_pairs={{1,0},{2,1},{3,2},{5,4},{6,5},{7,6},{9,8},{10,9},{11,10},{13,12},{... | collective-permute-start | bytes 135176 | tf_op jit(solution)/shard_map/ppermute | solution.py:51
where the time goes:
time: 390 us; the launch traced here: 389 us
  local copies, waits for them, and re-layouts  316 us (81%)
  other arithmetic  31.9 us (8%)
  starting transfers between devices  24.4 us (6%)
  waiting for transfers between devices  15.4 us (4%)
    gather x8, local copies, waits for them, and re-layouts, gather_corners(): jnp.take(flat_state, corner_base + shift[0] * stride_x + shift[1] * strid...  250 us
    scatter x1, local copies, waits for them, and re-layouts, per_device(): flat_state.at[:, targets].set(received.reshape(var_count, -1), mode='drop')  27.4 us
    another operation x1, other arithmetic, joined_exchange(): blocks = jnp.moveaxis(in_blocks(blocks, splits[1] + 1, sizes[1]), 0, 1)  23.1 us
    all_to_all x1, starting transfers between devices, joined_exchange(): lax.all_to_all(blocks, axis, split_axis=0, concat_axis=0, tiled=True)  15.6 us
    all_to_all x1, waiting for transfers between devices, joined_exchange(): lax.all_to_all(blocks, axis, split_axis=0, concat_axis=0, tiled=True)  15.4 us
    slice x2, local copies, waits for them, and re-layouts, advance(): magnetic[:, 1:-1, 1:-1, 1:-1]  11.8 us
  transfers between devices with their start and end apart: 5, of which 1 were waited for; matrix products, arithmetic and copies ran while one was open for 4% of the time, Pallas kernels for 0%

commit v1 on v0

v1 whole, which is shorter than its diff:
```python
import jax
import jax.numpy as jnp
from jax import lax
from jax.experimental import pallas as pl
from jax.experimental.pallas import tpu as pltpu
from jax.sharding import PartitionSpec as P

signal_speed = 0.5
courant_number = 0.3
f32 = jnp.float32
bf16 = jnp.bfloat16
MESH = pl.DeviceIdType.MESH
VMEM = pl.BlockSpec(memory_space=pltpu.VMEM)


def halves(x):
    head = x.astype(bf16)
    return head, (x - head.astype(f32)).astype(bf16)


def grid_step(k):
    return 1 + lax.rem(k + 1, 3)


def packed_rows(block):
    return jnp.concatenate([block[0:8], block[16:24], block[8:16], block[24:32]], axis=1)


def gather_kernel(state_ref, corner_ref, frac_ref, out_ref, lhs, ints, floats, prod, turned):
    g = lax.axis_index("grp")
    head, rest = halves(state_ref[...])
    lhs[:, 0:128] = head
    lhs[:, 128:256] = rest

    @pl.loop(0, 3)
    def _(k):
        h = lax.rem(g + grid_step(k), 4)
        ints[...] = packed_rows(corner_ref[h])
        for d in range(3):
            floats[d] = packed_rows(frac_ref[d, h])

        @pl.loop(0, 8)
        def _(rr):
            base = ints[pl.ds(rr, 1), :]
            fx = floats[0, pl.ds(rr, 1), :]
            fy = floats[1, pl.ds(rr, 1), :]
            fz = floats[2, pl.ds(rr, 1), :]
            cz = base & 127
            cy = (base >> 7) & 15
            cx = base >> 11
            iz = lax.broadcasted_iota(jnp.int32, (128, 256), 0)
            wz = jnp.where(iz == cz, 1.0 - fz, jnp.where(iz == cz + 1, fz, 0.0))
            z_head, z_rest = halves(wz)
            both = lhs[...]
            prod[...] = jnp.dot(
                both, jnp.concatenate([z_head, z_head], axis=0), preferred_element_type=f32
            ) + jnp.dot(both, jnp.concatenate([z_rest, z_rest], axis=0), preferred_element_type=f32)
            iy = lax.broadcasted_iota(jnp.int32, (16, 256), 0)
            wy = jnp.where(iy == cy, 1.0 - fy, jnp.where(iy == cy + 1, fy, 0.0))
            wx = [jnp.where(cx == x, 1.0 - fx, jnp.where(cx + 1 == x, fx, 0.0)) for x in range(8)]
            rows = []
            for v in range(8):
                total = prod[v * 128 : v * 128 + 16, :] * wx[0]
                for x in range(1, 8):
                    start = v * 128 + x * 16
                    total = total + prod[start : start + 16, :] * wx[x]
                rows.append(jnp.sum(total * wy, axis=0, keepdims=True))
            values = jnp.concatenate(rows, axis=0)
            turned[pl.ds(pl.multiple_of(rr * 8, 8), 8), :] = values[:, 0:128]
            turned[pl.ds(pl.multiple_of(64 + rr * 8, 8), 8), :] = values[:, 128:256]

        out_ref[k] = turned[...].T


def gather(state, corner, frac):
    return pl.pallas_call(
        gather_kernel,
        out_shape=jax.ShapeDtypeStruct((3, 128, 128), f32),
        in_specs=[VMEM] * 3,
        out_specs=VMEM,
        scratch_shapes=[
            pltpu.VMEM((1024, 256), bf16),
            pltpu.VMEM((8, 256), jnp.int32),
            pltpu.VMEM((3, 8, 256), f32),
            pltpu.VMEM((1024, 256), f32),
            pltpu.VMEM((128, 128), f32),
        ],
        name="gather",
    )(state, corner, frac)


def side_copies(face_x, face_y, land_x, land_y, send, recv):
    i, j = lax.axis_index("gx"), lax.axis_index("gy")
    up_x, down_x = lax.rem(i + 1, 16), lax.rem(i + 15, 16)
    up_y, down_y = lax.rem(j + 1, 4), lax.rem(j + 3, 4)
    copies = []
    for n, (src, dst, where) in enumerate(
        (
            (face_x.at[:, 7], land_x.at[0], {"gx": up_x}),
            (face_x.at[:, 0], land_x.at[1], {"gx": down_x}),
            (face_y.at[1], land_y.at[0], {"gy": up_y}),
            (face_y.at[0], land_y.at[1], {"gy": down_y}),
        )
    ):
        copies.append(
            pltpu.make_async_remote_copy(
                src_ref=src,
                dst_ref=dst,
                send_sem=send.at[n],
                recv_sem=recv.at[n],
                device_id=where,
                device_id_type=MESH,
            )
        )
    return copies


def greet_sides(barrier):
    i, j = lax.axis_index("gx"), lax.axis_index("gy")
    for where in (
        {"gx": lax.rem(i + 1, 16)},
        {"gx": lax.rem(i + 15, 16)},
        {"gy": lax.rem(j + 1, 4)},
        {"gy": lax.rem(j + 3, 4)},
    ):
        pl.semaphore_signal(barrier, inc=1, device_id=where, device_id_type=MESH)


def exchange_kernel(
    out_vals, vel_ref, in_vals, vel_x, vel_y, face_y, send, recv, side_send, side_recv
):
    g, i, j = lax.axis_index("grp"), lax.axis_index("gx"), lax.axis_index("gy")
    me = i * 4 + j
    barrier = pltpu.get_barrier_semaphore()

    @pl.loop(0, 192)
    def _(n):
        k, q = n // 64, lax.rem(n, 64)
        where = {"grp": lax.rem(g + grid_step(k), 4), "gx": q // 4, "gy": lax.rem(q, 4)}
        pl.semaphore_signal(barrier, inc=1, device_id=where, device_id_type=MESH)

    greet_sides(barrier)
    face_y[0] = vel_ref[:, :, 0, :]
    face_y[1] = vel_ref[:, :, 15, :]
    pl.semaphore_wait(barrier, 196)

    @pl.loop(0, 192)
    def _(n):
        k, q = n // 64, lax.rem(n, 64)
        where = {"grp": lax.rem(g + grid_step(k), 4), "gx": q // 4, "gy": lax.rem(q, 4)}
        pltpu.make_async_remote_copy(
            src_ref=out_vals.at[k, :, q],
            dst_ref=in_vals.at[k, :, me],
            send_sem=send,
            recv_sem=recv,
            device_id=where,
            device_id_type=MESH,
        ).start()

    sides = side_copies(vel_ref, face_y, vel_x, vel_y, side_send, side_recv)
    for copy in sides:
        copy.start()
    whole = pltpu.make_async_remote_copy(
        src_ref=out_vals,
        dst_ref=in_vals,
        send_sem=send,
        recv_sem=recv,
        device_id={"gx": lax.rem(i + 1, 16)},
        device_id_type=MESH,
    )
    whole.wait_send()
    whole.wait_recv()
    for copy in sides:
        copy.wait()


def exchange(out_vals, velocity):
    return pl.pallas_call(
        exchange_kernel,
        out_shape=(
            jax.ShapeDtypeStruct((3, 2, 64, 1, 128), f32),
            jax.ShapeDtypeStruct((2, 3, 16, 128), f32),
            jax.ShapeDtypeStruct((2, 3, 8, 128), f32),
        ),
        in_specs=[VMEM] * 2,
        out_specs=(VMEM,) * 3,
        scratch_shapes=[
            pltpu.VMEM((2, 3, 8, 128), f32),
            pltpu.SemaphoreType.DMA,
            pltpu.SemaphoreType.DMA,
            pltpu.SemaphoreType.DMA((4,)),
            pltpu.SemaphoreType.DMA((4,)),
        ],
        compiler_params=pltpu.CompilerParams(collective_id=0, has_side_effects=True),
        name="exchange",
    )(out_vals, velocity)


def place_kernel(
    vals_ref, target_ref, state_ref, filled, land_x, land_y, lhs, rhs, acc, ints, turned, face_y,
    send, recv,
):
    g = lax.axis_index("grp")
    barrier = pltpu.get_barrier_semaphore()
    greet_sides(barrier)
    acc[...] = jnp.zeros_like(acc)

    @pl.loop(0, 3)
    def _(k):
        source = lax.rem(g + 4 - grid_step(k), 4)
        ints[...] = packed_rows(target_ref[source])
        turned[...] = vals_ref[k].T

        @pl.loop(0, 8)
        def _(rr):
            cell = ints[pl.ds(rr, 1), :]
            column = cell >> 7
            row = column & 31
            lane = ((column >> 6) << 7) + (((cell & 127) + ((column & 32) << 1)) & 127)
            values = jnp.concatenate(
                [
                    turned[pl.ds(pl.multiple_of(rr * 8, 8), 8), :],
                    turned[pl.ds(pl.multiple_of(64 + rr * 8, 8), 8), :],
                ],
                axis=1,
            )
            head = values.astype(bf16).astype(f32)
            rest = values - head
            hit = lax.broadcasted_iota(jnp.int32, (32, 256), 0) == row
            at = pl.ds(pl.multiple_of(rr * 256, 256), 256)
            for v in range(8):
                lhs[v * 32 : v * 32 + 32, at] = jnp.where(hit, head[v : v + 1, :], 0.0).astype(bf16)
                lhs[256 + v * 32 : 288 + v * 32, at] = jnp.where(
                    hit, rest[v : v + 1, :], 0.0
                ).astype(bf16)
            lhs[512:544, at] = jnp.where(hit, 1.0, 0.0).astype(bf16)
            il = lax.broadcasted_iota(jnp.int32, (256, 256), 0)
            rhs[:, at] = jnp.where(il == lane, 1.0, 0.0).astype(bf16)

        acc[...] += lax.dot_general(
            lhs[...], rhs[...], (((1,), (1,)), ((), ())), preferred_element_type=f32
        )

    spot = lax.broadcasted_iota(jnp.int32, (32, 128), 1)
    rim = (spot < 32) | (spot >= 96)
    for pair in range(2):
        span = slice(pair * 128, pair * 128 + 128)
        count = acc[512:544, span]
        for b in range(2):
            seen = pltpu.roll(count, 64, 1) if b else count
            hit = rim & (seen > 0.5)
            x = 4 * pair + 2 * b
            for v in range(8):
                new = acc[v * 32 : v * 32 + 32, span] + acc[256 + v * 32 : 288 + v * 32, span]
                if b:
                    new = pltpu.roll(new, 64, 1)
                old = state_ref[v, x : x + 2].reshape(32, 128)
                filled[v, x : x + 2] = jnp.where(hit, new, old).reshape(2, 16, 128)
    face_y[0] = filled[:, :, 0, :]
    face_y[1] = filled[:, :, 15, :]
    pl.semaphore_wait(barrier, 4)
    sides = side_copies(filled, face_y, land_x, land_y, send, recv)
    for copy in sides:
        copy.start()
    for copy in sides:
        copy.wait()


def place(vals, target, state):
    return pl.pallas_call(
        place_kernel,
        out_shape=(
            jax.ShapeDtypeStruct((8, 8, 16, 128), f32),
            jax.ShapeDtypeStruct((2, 8, 16, 128), f32),
            jax.ShapeDtypeStruct((2, 8, 8, 128), f32),
        ),
        in_specs=[VMEM] * 3,
        out_specs=(VMEM,) * 3,
        scratch_shapes=[
            pltpu.VMEM((544, 2048), bf16),
            pltpu.VMEM((256, 2048), bf16),
            pltpu.VMEM((544, 256), f32),
            pltpu.VMEM((8, 256), jnp.int32),
            pltpu.VMEM((128, 128), f32),
            pltpu.VMEM((2, 8, 8, 128), f32),
            pltpu.SemaphoreType.DMA((4,)),
            pltpu.SemaphoreType.DMA((4,)),
        ],
        compiler_params=pltpu.CompilerParams(collective_id=1, has_side_effects=True),
        name="place",
    )(vals, target, state)


def face_weights(low, high):
    wave_low = jnp.minimum(jnp.minimum(low, high) - signal_speed, 0.0)
    wave_high = jnp.maximum(jnp.maximum(low, high) + signal_speed, 0.0)
    scale = courant_number / (wave_high - wave_low)
    return (
        wave_high * (low - wave_low) * scale,
        wave_low * (wave_high - high) * scale,
    )


def step_kernel(u_ref, vel_ref, ux_ref, uy_ref, vx_ref, vy_ref, out_ref):
    i, j = lax.axis_index("gx"), lax.axis_index("gy")
    lane = lax.broadcasted_iota(jnp.int32, (16, 128), 1)
    line = lax.broadcasted_iota(jnp.int32, (16, 128), 0)
    keep_low_x, keep_high_x = i > 0, i < 15
    keep_low_y, keep_high_y = j > 0, j < 3

    def plane(ref, side, v, x):
        if x < 0:
            return jnp.where(keep_low_x, side[0, v], 0.0)
        if x > 7:
            return jnp.where(keep_high_x, side[1, v], 0.0)
        return ref[v, x]

    def row(side, which, v, x):
        keep = keep_high_y if which else keep_low_y
        return jnp.where(keep, side[which, v, x : x + 1, :], 0.0)

    def prev_z(a):
        return jnp.where(lane == 0, 0.0, pltpu.roll(a, 1, 1))

    def next_z(a):
        return jnp.where(lane == 127, 0.0, pltpu.roll(a, 127, 1))

    def prev_y(a, low):
        return jnp.where(line == 0, low, pltpu.roll(a, 1, 0))

    def next_y(a, high):
        return jnp.where(line == 15, high, pltpu.roll(a, 15, 0))

    def elec(b, v):
        return (v[2] * b[1] - v[1] * b[2], v[0] * b[2] - v[2] * b[0], v[1] * b[0] - v[0] * b[1])

    speed = [[plane(vel_ref, vx_ref, d, x) for d in range(3)] for x in range(-1, 9)]
    weights_x = [face_weights(speed[x][0], speed[x + 1][0]) for x in range(9)]
    fields = [
        elec([plane(u_ref, ux_ref, 5 + d, x) for d in range(3)], speed[x + 1]) for x in range(-1, 9)
    ]
    flux_low = [
        weights_x[0][0] * plane(u_ref, ux_ref, v, -1) + weights_x[0][1] * u_ref[v, 0]
        for v in range(5)
    ]
    for x in range(8):
        here = speed[x + 1]
        low_v = [row(vy_ref, 0, d, x) for d in range(3)]
        high_v = [row(vy_ref, 1, d, x) for d in range(3)]
        y_low = face_weights(prev_y(here[1], low_v[1]), here[1])
        y_high = face_weights(here[1], next_y(here[1], high_v[1]))
        z_low = face_weights(prev_z(here[2]), here[2])
        z_high = face_weights(here[2], next_z(here[2]))
        centre = (
            1.0
            + y_low[1] - y_high[0]
            + z_low[1] - z_high[0]
        )
        for v in range(5):
            u = u_ref[v, x]
            flux_high = weights_x[x + 1][0] * u + weights_x[x + 1][1] * plane(
                u_ref, ux_ref, v, x + 1
            )
            new = centre * u - (flux_high - flux_low[v])
            flux_low[v] = flux_high
            new = new + y_low[0] * prev_y(u, row(uy_ref, 0, v, x))
            new = new - y_high[1] * next_y(u, row(uy_ref, 1, v, x))
            new = new + z_low[0] * prev_z(u)
            new = new - z_high[1] * next_z(u)
            out_ref[v, x] = new
        below, e, above = fields[x], fields[x + 1], fields[x + 2]
        e_low = elec([row(uy_ref, 0, 5 + d, x) for d in range(3)], low_v)
        e_high = elec([row(uy_ref, 1, 5 + d, x) for d in range(3)], high_v)

        def along_y(d):
            return next_y(e[d], e_high[d]) - prev_y(e[d], e_low[d])

        def along_z(d):
            return next_z(e[d]) - prev_z(e[d])

        def along_x(d):
            return above[d] - below[d]

        half = 0.5 * courant_number
        out_ref[5, x] = u_ref[5, x] - half * (along_y(2) - along_z(1))
        out_ref[6, x] = u_ref[6, x] - half * (along_z(0) - along_x(2))
        out_ref[7, x] = u_ref[7, x] - half * (along_x(1) - along_y(0))


def step(u, vel, ux, uy, vx, vy):
    return pl.pallas_call(
        step_kernel,
        out_shape=jax.ShapeDtypeStruct((8, 8, 16, 128), f32),
        in_specs=[VMEM] * 6,
        out_specs=VMEM,
        name="step",
    )(u, vel, ux, uy, vx, vy)


def per_device(conserved, velocity, donor_corner, donor_fraction, target_cell):
    state = conserved[:, 0]
    speeds = velocity[:, 0]
    corner = donor_corner[0, 0, 0].transpose(0, 2, 1)
    frac = donor_fraction[:, 0, 0, 0].transpose(0, 1, 3, 2)
    target = target_cell[0, 0, 0].transpose(0, 2, 1)
    sent = gather(state.reshape(1024, 128), corner, frac)
    came, vel_x, vel_y = exchange(sent.reshape(3, 2, 64, 1, 128), speeds)
    filled, u_x, u_y = place(came.reshape(3, 128, 128), target, state)
    return step(filled, speeds, u_x, u_y, vel_x, vel_y)[:, None]


def solution(mesh):
    return jax.shard_map(
        per_device,
        mesh=mesh,
        in_specs=(
            P(None, "grp", "gx", "gy", None),
            P(None, "grp", "gx", "gy", None),
            P("grp", "gx", "gy", None, None, None),
            P(None, "grp", "gx", "gy", None, None, None),
            P("grp", "gx", "gy", None, None, None),
        ),
        out_specs=P(None, "grp", "gx", "gy", None),
        check_vma=False,
    )
```

time: 390 us -> 54.8 us (0.14)
  local copies, waits for them, and re-layouts: 316 us -> 0 us
  Pallas kernels: 0 us -> 53.7 us
  other arithmetic: 31.9 us -> 0 us
  starting transfers between devices: 24.4 us -> 0 us
  waiting for transfers between devices: 15.4 us -> 0 us
    gather x8 -> x0, local copies, waits for them, and re-layouts: 250 us -> none  [gather_corners(): jnp.take(flat_state, corner_base + shift[0] * stride_x + shift[1] * strid...]
    pallas_call x0 -> x4, Pallas kernels: none -> 53.7 us  [the longest x1 27.5 us: exchange(): pl.pallas_call(exchange_kernel, out_shape=(jax.ShapeDtypeStruct((3, 2, 64...]
    scatter x1 -> x0, local copies, waits for them, and re-layouts: 27.4 us -> none  [per_device(): flat_state.at[:, targets].set(received.reshape(var_count, -1), mode='drop')]
    another operation x2 -> x0, other arithmetic: 23.4 us -> none  [the longest x1 23.1 us: joined_exchange(): blocks = jnp.moveaxis(in_blocks(blocks, splits[1] + 1, sizes[1]), 0, 1)]
    slice x3 -> x0, local copies, waits for them, and re-layouts: 17.1 us -> none  [the longest x2 11.8 us: advance(): magnetic[:, 1:-1, 1:-1, 1:-1]]
    all_to_all x1 -> x0, starting transfers between devices: 15.6 us -> none  [joined_exchange(): lax.all_to_all(blocks, axis, split_axis=0, concat_axis=0, tiled=True)]
    all_to_all x1 -> x0, waiting for transfers between devices: 15.4 us -> none  [joined_exchange(): lax.all_to_all(blocks, axis, split_axis=0, concat_axis=0, tiled=True)]
    ppermute x4 -> x0, starting transfers between devices: 8.76 us -> none  [the longest x2 5.37 us: extended(): lax.ppermute(last, axis, up)]
  transfers between devices with their start and end apart: 5 -> 0, of which waited for: 1 -> 0; matrix products, arithmetic and copies ran while one was open for 4% -> 0% of each run, Pallas kernels for 0% -> 0%
where the time goes in v1:
time: 54.8 us; the launch traced here: 53.7 us
  Pallas kernels  53.7 us (98%)
    pallas_call x1, Pallas kernels, exchange(): pl.pallas_call(exchange_kernel, out_shape=(jax.ShapeDtypeStruct((3, 2, 64...  27.5 us
    pallas_call x1, Pallas kernels, gather(): pl.pallas_call(gather_kernel, out_shape=jax.ShapeDtypeStruct((3, 128, 128...  13.7 us
    pallas_call x1, Pallas kernels, place(): pl.pallas_call(place_kernel, out_shape=(jax.ShapeDtypeStruct((8, 8, 16, 1...  10 us
    pallas_call x1, Pallas kernels, step(): pl.pallas_call(step_kernel, out_shape=jax.ShapeDtypeStruct((8, 8, 16, 128...  2.56 us

profile of v1, /device:TPU:1, one launch (start us, length us, event | category | flops | bytes accessed | tf_op | source)
XLA Modules:
  0.0 53.7 jit_solution(11590620760479004331)
XLA Ops:
  0.0 13.7 %gather.1 = f32[3,128,128]{2,1,0:T(8,128)} custom-call(f32[1024,128]{1,0:T(8,128)} %bitcast.17, s32[4,32,64]{2,1,0:T(8,128)} %bitcast.25, f32[3,4,32,64]{3,2,1,0:T(8,128)} %bitcast.23), custom_call_target="tpu_custom_call" | custom-call | tf_op jit(solution)/shard_map/gather/pallas_call | solution.py:76
  13.7 27.5 %exchange.1 = (f32[3,2,64,1,128]{4,3,2,1,0:T(1,128)}, f32[2,3,16,128]{3,2,1,0:T(8,128)}, f32[2,3,8,128]{3,2,1,0:T(8,128)}) custom-call(f32[3,2,64,1,128]{4,3,2,1,0:T(1,128)} %bitcast.21, f32[3,8,16,128]{3,2,1,0:T(8,128)} %bitcast.19), custom_call_target="tpu_custom_call" | custom-call | tf_op jit(solution)/shard_map/exchange/pallas_call | solution.py:178
  41.2 10.0 %place.1 = (f32[8,8,16,128]{3,2,1,0:T(8,128)}, f32[2,8,16,128]{3,2,1,0:T(8,128)}, f32[2,8,8,128]{3,2,1,0:T(8,128)}) custom-call(f32[3,128,128]{2,1,0:T(8,128)} %bitcast.22, s32[4,32,64]{2,1,0:T(8,128)} %bitcast.24, f32[8,8,16,128]{3,2,1,0:T(8,128)} %bitcast.18), custom_call_target="tpu_custom_call" | custom-call | tf_op jit(solution)/shard_map/place/pallas_call | solution.py:270
  51.2 2.6 %step.1 = f32[8,8,16,128]{3,2,1,0:T(8,128)} custom-call(f32[8,8,16,128]{3,2,1,0:T(8,128)} %get-tuple-element.12.u_ref, f32[3,8,16,128]{3,2,1,0:T(8,128)} %bitcast.20, f32[2,8,16,128]{3,2,1,0:T(8,128)} %get-tuple-element.13.ux_ref, f32[2,8,8,128]{3,2,1,0:T(8,128)} %get-tuple-element.14.uy_ref, f32[2,3,16,128]{3,2,1,0:T(8,128)} %get-tuple-element.15.vx_ref, ...), custom_call_target="tpu_custom_call" | custom-call | tf_op jit(solution)/shard_map/step/pallas_call | solution.py:391

commit v2 on v1

v2 whole, which is shorter than its diff:
```python
import jax
import jax.numpy as jnp
from jax import lax
from jax.experimental import pallas as pl
from jax.experimental.pallas import tpu as pltpu
from jax.sharding import PartitionSpec as P

signal_speed = 0.5
courant_number = 0.3
f32 = jnp.float32
bf16 = jnp.bfloat16
MESH = pl.DeviceIdType.MESH
VMEM = pl.BlockSpec(memory_space=pltpu.VMEM)


def halves(x):
    head = x.astype(bf16)
    return head, (x - head.astype(f32)).astype(bf16)


def grid_step(k):
    return 1 + lax.rem(k + 1, 3)


def packed_rows(block):
    return jnp.concatenate([block[0:8], block[16:24], block[8:16], block[24:32]], axis=1)


def neighbours():
    i, j = lax.axis_index("gx"), lax.axis_index("gy")
    return (
        {"gx": lax.rem(i + 1, 16)},
        {"gx": lax.rem(i + 15, 16)},
        {"gy": lax.rem(j + 1, 4)},
        {"gy": lax.rem(j + 3, 4)},
    )


def side_copies(face_x, face_y, land_x, land_y, send, recv):
    pairs = (
        (face_x.at[:, 7], land_x.at[0]),
        (face_x.at[:, 0], land_x.at[1]),
        (face_y.at[1], land_y.at[0]),
        (face_y.at[0], land_y.at[1]),
    )
    return [
        remote(src, dst, send.at[n], recv.at[n], where)
        for n, ((src, dst), where) in enumerate(zip(pairs, neighbours()))
    ]


def remote(src, dst, send, recv, where):
    return pltpu.make_async_remote_copy(
        src_ref=src,
        dst_ref=dst,
        send_sem=send,
        recv_sem=recv,
        device_id=where,
        device_id_type=MESH,
    )


def interpolate(rr, lhs, ints, floats, prod, turned):
    base = ints[pl.ds(rr, 1), :]
    fx = floats[0, pl.ds(rr, 1), :]
    fy = floats[1, pl.ds(rr, 1), :]
    fz = floats[2, pl.ds(rr, 1), :]
    cz = base & 127
    cy = (base >> 7) & 15
    cx = base >> 11
    iz = lax.broadcasted_iota(jnp.int32, (128, 256), 0)
    wz = jnp.where(iz == cz, 1.0 - fz, jnp.where(iz == cz + 1, fz, 0.0))
    z_head, z_rest = halves(wz)
    both = lhs[...]
    prod[...] = jnp.dot(
        both, jnp.concatenate([z_head, z_head], axis=0), preferred_element_type=f32
    ) + jnp.dot(both, jnp.concatenate([z_rest, z_rest], axis=0), preferred_element_type=f32)
    iy = lax.broadcasted_iota(jnp.int32, (16, 256), 0)
    wy = jnp.where(iy == cy, 1.0 - fy, jnp.where(iy == cy + 1, fy, 0.0))
    wx = [jnp.where(cx == x, 1.0 - fx, jnp.where(cx + 1 == x, fx, 0.0)) for x in range(8)]
    rows = []
    for v in range(8):
        total = prod[v * 128 : v * 128 + 16, :] * wx[0]
        for x in range(1, 8):
            start = v * 128 + x * 16
            total = total + prod[start : start + 16, :] * wx[x]
        rows.append(jnp.sum(total * wy, axis=0, keepdims=True))
    values = jnp.concatenate(rows, axis=0)
    turned[pl.ds(pl.multiple_of(rr * 8, 8), 8), :] = values[:, 0:128]
    turned[pl.ds(pl.multiple_of(64 + rr * 8, 8), 8), :] = values[:, 128:256]


def spots(ints, rr):
    cell = ints[pl.ds(rr, 1), :]
    column = cell >> 7
    lane = ((column >> 6) << 7) + (((cell & 127) + ((column & 32) << 1)) & 127)
    return column & 31, lane


def section_kernel(
    state_ref, vel_ref, corner_ref, frac_ref, target_ref,
    filled, u_x, u_y, v_x, v_y,
    lhs, ints, floats, prods, turned, first, second, third, put_rows, put_lanes, acc, cells,
    face_u, face_v,
    y_send, y_recv, d_send, d_recv, v_send, v_recv, u_send, u_recv,
):
    g, i, j = lax.axis_index("grp"), lax.axis_index("gx"), lax.axis_index("gy")
    barrier = pltpu.get_barrier_semaphore()

    @pl.loop(0, 48)
    def _(n):
        where = {"grp": lax.rem(g + 1 + n // 16, 4), "gx": lax.rem(n, 16)}
        pl.semaphore_signal(barrier, inc=1, device_id=where, device_id_type=MESH)

    for d in range(1, 4):
        where = {"gy": lax.rem(j + d, 4)}
        pl.semaphore_signal(barrier, inc=1, device_id=where, device_id_type=MESH)
    for where in neighbours()[:2]:
        pl.semaphore_signal(barrier, inc=1, device_id=where, device_id_type=MESH)

    head, rest = halves(state_ref[...].reshape(1024, 128))
    lhs[:, 0:128] = head
    lhs[:, 128:256] = rest
    face_v[0] = vel_ref[:, :, 0, :]
    face_v[1] = vel_ref[:, :, 15, :]
    v_sides = side_copies(vel_ref, face_v, v_x, v_y, v_send, v_recv)

    def onward(k):
        some = first.at[0, :, :, 0:3]
        remote(some, second.at[k, :, :, 0:3], y_send, y_recv.at[k], {"gx": i}).wait_recv()

        @pl.loop(0, 16)
        def _(to):
            where = {"grp": lax.rem(g + grid_step(k), 4), "gx": to}
            remote(second.at[k, :, to], third.at[k, :, i], d_send, d_recv.at[k], where).start()

    @pl.loop(0, 3)
    def _(k):
        h = lax.rem(g + grid_step(k), 4)
        ints[...] = packed_rows(corner_ref[h])
        for d in range(3):
            floats[d] = packed_rows(frac_ref[d, h])

        @pl.loop(0, 8 // len(prods))
        def _(step):
            for n, prod in enumerate(prods):
                interpolate(step * len(prods) + n, lhs, ints, floats, prod, turned)

        first[k] = turned[...].T.reshape(2, 16, 4, 1, 128)
        second[k, :, :, j] = first[k, :, :, j]

        @pl.when(k == 0)
        def _():
            pl.semaphore_wait(barrier, 53)

        for d in range(1, 4):
            to = lax.rem(j + d, 4)
            remote(
                first.at[k, :, :, to], second.at[k, :, :, j], y_send, y_recv.at[k], {"gy": to}
            ).start()

        @pl.when(k == 0)
        def _():
            for copy in v_sides:
                copy.start()

        @pl.when(k > 0)
        def _():
            onward(k - 1)

    @pl.loop(0, 3)
    def _(k):
        cells[k] = packed_rows(target_ref[lax.rem(g + 4 - grid_step(k), 4)])

    onward(2)

    @pl.loop(0, 24)
    def _(n):
        k, rr = n // 8, lax.rem(n, 8)
        _, lane = spots(cells.at[k], rr)
        il = lax.broadcasted_iota(jnp.int32, (256, 256), 0)
        put_lanes[:, pl.ds(pl.multiple_of(n * 256, 256), 256)] = jnp.where(
            il == lane, 1.0, 0.0
        ).astype(bf16)

    acc[...] = jnp.zeros_like(acc)

    @pl.loop(0, 3)
    def _(k):
        remote(second.at[k], third.at[k], d_send, d_recv.at[k], {"gx": i}).wait_recv()
        turned[...] = third[k].reshape(128, 128).T

        @pl.loop(0, 8)
        def _(rr):
            row, _ = spots(cells.at[k], rr)
            values = jnp.concatenate(
                [
                    turned[pl.ds(pl.multiple_of(rr * 8, 8), 8), :],
                    turned[pl.ds(pl.multiple_of(64 + rr * 8, 8), 8), :],
                ],
                axis=1,
            )
            head = values.astype(bf16).astype(f32)
            rest = values - head
            hit = lax.broadcasted_iota(jnp.int32, (32, 256), 0) == row
            at = pl.ds(pl.multiple_of(rr * 256, 256), 256)
            for v in range(8):
                put_rows[v * 32 : v * 32 + 32, at] = jnp.where(hit, head[v : v + 1, :], 0.0).astype(
                    bf16
                )
                put_rows[256 + v * 32 : 288 + v * 32, at] = jnp.where(
                    hit, rest[v : v + 1, :], 0.0
                ).astype(bf16)
            put_rows[512:544, at] = jnp.where(hit, 1.0, 0.0).astype(bf16)

        acc[...] += lax.dot_general(
            put_rows[...],
            put_lanes[:, pl.ds(pl.multiple_of(k * 2048, 2048), 2048)],
            (((1,), (1,)), ((), ())),
            preferred_element_type=f32,
        )

    spot = lax.broadcasted_iota(jnp.int32, (32, 128), 1)
    rim = (spot < 32) | (spot >= 96)
    for pair in range(2):
        span = slice(pair * 128, pair * 128 + 128)
        count = acc[512:544, span]
        for b in range(2):
            seen = pltpu.roll(count, 64, 1) if b else count
            hit = rim & (seen > 0.5)
            x = 4 * pair + 2 * b
            for v in range(8):
                new = acc[v * 32 : v * 32 + 32, span] + acc[256 + v * 32 : 288 + v * 32, span]
                if b:
                    new = pltpu.roll(new, 64, 1)
                old = state_ref[v, x : x + 2].reshape(32, 128)
                filled[v, x : x + 2] = jnp.where(hit, new, old).reshape(2, 16, 128)
    face_u[0] = filled[:, :, 0, :]
    face_u[1] = filled[:, :, 15, :]
    u_sides = side_copies(filled, face_u, u_x, u_y, u_send, u_recv)
    for copy in u_sides:
        copy.start()
    for copy in v_sides + u_sides:
        copy.wait()
    remote(first.at[:, :, :, 0:3], second.at[:, :, :, 0:3], y_send, y_recv.at[0], {"gx": i}).wait_send()
    remote(second, third, d_send, d_recv.at[0], {"gx": i}).wait_send()


UNROLL = 2


def section(state, velocity, corner, frac, target):
    dma = pltpu.SemaphoreType.DMA
    chunk = pltpu.VMEM((3, 2, 16, 4, 1, 128), f32)
    return pl.pallas_call(
        section_kernel,
        out_shape=(
            jax.ShapeDtypeStruct((8, 8, 16, 128), f32),
            jax.ShapeDtypeStruct((2, 8, 16, 128), f32),
            jax.ShapeDtypeStruct((2, 8, 8, 128), f32),
            jax.ShapeDtypeStruct((2, 3, 16, 128), f32),
            jax.ShapeDtypeStruct((2, 3, 8, 128), f32),
        ),
        in_specs=[VMEM] * 5,
        out_specs=(VMEM,) * 5,
        scratch_shapes=[
            pltpu.VMEM((1024, 256), bf16),
            pltpu.VMEM((8, 256), jnp.int32),
            pltpu.VMEM((3, 8, 256), f32),
            [pltpu.VMEM((1024, 256), f32) for _ in range(UNROLL)],
            pltpu.VMEM((128, 128), f32),
            chunk,
            chunk,
            chunk,
            pltpu.VMEM((544, 2048), bf16),
            pltpu.VMEM((256, 6144), bf16),
            pltpu.VMEM((544, 256), f32),
            pltpu.VMEM((3, 8, 256), jnp.int32),
            pltpu.VMEM((2, 8, 8, 128), f32),
            pltpu.VMEM((2, 3, 8, 128), f32),
            dma,
            dma((3,)),
            dma,
            dma((3,)),
            dma((4,)),
            dma((4,)),
            dma((4,)),
            dma((4,)),
        ],
        compiler_params=pltpu.CompilerParams(collective_id=0, has_side_effects=True),
        name="section",
    )(state, velocity, corner, frac, target)


def face_weights(low, high):
    wave_low = jnp.minimum(jnp.minimum(low, high) - signal_speed, 0.0)
    wave_high = jnp.maximum(jnp.maximum(low, high) + signal_speed, 0.0)
    scale = courant_number / (wave_high - wave_low)
    return (
        wave_high * (low - wave_low) * scale,
        wave_low * (wave_high - high) * scale,
    )


def step_kernel(u_ref, vel_ref, ux_ref, uy_ref, vx_ref, vy_ref, out_ref):
    i, j = lax.axis_index("gx"), lax.axis_index("gy")
    lane = lax.broadcasted_iota(jnp.int32, (16, 128), 1)
    line = lax.broadcasted_iota(jnp.int32, (16, 128), 0)
    keep_low_x, keep_high_x = i > 0, i < 15
    keep_low_y, keep_high_y = j > 0, j < 3

    def plane(ref, side, v, x):
        if x < 0:
            return jnp.where(keep_low_x, side[0, v], 0.0)
        if x > 7:
            return jnp.where(keep_high_x, side[1, v], 0.0)
        return ref[v, x]

    def row(side, which, v, x):
        keep = keep_high_y if which else keep_low_y
        return jnp.where(keep, side[which, v, x : x + 1, :], 0.0)

    def prev_z(a):
        return jnp.where(lane == 0, 0.0, pltpu.roll(a, 1, 1))

    def next_z(a):
        return jnp.where(lane == 127, 0.0, pltpu.roll(a, 127, 1))

    def prev_y(a, low):
        return jnp.where(line == 0, low, pltpu.roll(a, 1, 0))

    def next_y(a, high):
        return jnp.where(line == 15, high, pltpu.roll(a, 15, 0))

    def elec(b, v):
        return (v[2] * b[1] - v[1] * b[2], v[0] * b[2] - v[2] * b[0], v[1] * b[0] - v[0] * b[1])

    speed = [[plane(vel_ref, vx_ref, d, x) for d in range(3)] for x in range(-1, 9)]
    weights_x = [face_weights(speed[x][0], speed[x + 1][0]) for x in range(9)]
    fields = [
        elec([plane(u_ref, ux_ref, 5 + d, x) for d in range(3)], speed[x + 1]) for x in range(-1, 9)
    ]
    flux_low = [
        weights_x[0][0] * plane(u_ref, ux_ref, v, -1) + weights_x[0][1] * u_ref[v, 0]
        for v in range(5)
    ]
    for x in range(8):
        here = speed[x + 1]
        low_v = [row(vy_ref, 0, d, x) for d in range(3)]
        high_v = [row(vy_ref, 1, d, x) for d in range(3)]
        y_low = face_weights(prev_y(here[1], low_v[1]), here[1])
        y_high = face_weights(here[1], next_y(here[1], high_v[1]))
        z_low = face_weights(prev_z(here[2]), here[2])
        z_high = face_weights(here[2], next_z(here[2]))
        centre = (
            1.0
            + y_low[1] - y_high[0]
            + z_low[1] - z_high[0]
        )
        for v in range(5):
            u = u_ref[v, x]
            flux_high = weights_x[x + 1][0] * u + weights_x[x + 1][1] * plane(
                u_ref, ux_ref, v, x + 1
            )
            new = centre * u - (flux_high - flux_low[v])
            flux_low[v] = flux_high
            new = new + y_low[0] * prev_y(u, row(uy_ref, 0, v, x))
            new = new - y_high[1] * next_y(u, row(uy_ref, 1, v, x))
            new = new + z_low[0] * prev_z(u)
            new = new - z_high[1] * next_z(u)
            out_ref[v, x] = new
        below, e, above = fields[x], fields[x + 1], fields[x + 2]
        e_low = elec([row(uy_ref, 0, 5 + d, x) for d in range(3)], low_v)
        e_high = elec([row(uy_ref, 1, 5 + d, x) for d in range(3)], high_v)

        def along_y(d):
            return next_y(e[d], e_high[d]) - prev_y(e[d], e_low[d])

        def along_z(d):
            return next_z(e[d]) - prev_z(e[d])

        def along_x(d):
            return above[d] - below[d]

        half = 0.5 * courant_number
        out_ref[5, x] = u_ref[5, x] - half * (along_y(2) - along_z(1))
        out_ref[6, x] = u_ref[6, x] - half * (along_z(0) - along_x(2))
        out_ref[7, x] = u_ref[7, x] - half * (along_x(1) - along_y(0))


def step(u, vel, ux, uy, vx, vy):
    return pl.pallas_call(
        step_kernel,
        out_shape=jax.ShapeDtypeStruct((8, 8, 16, 128), f32),
        in_specs=[VMEM] * 6,
        out_specs=VMEM,
        name="step",
    )(u, vel, ux, uy, vx, vy)


def per_device(conserved, velocity, donor_corner, donor_fraction, target_cell):
    state = conserved[:, 0]
    speeds = velocity[:, 0]
    corner = donor_corner[0, 0, 0].transpose(0, 2, 1)
    frac = donor_fraction[:, 0, 0, 0].transpose(0, 1, 3, 2)
    target = target_cell[0, 0, 0].transpose(0, 2, 1)
    filled, u_x, u_y, v_x, v_y = section(state, speeds, corner, frac, target)
    return step(filled, speeds, u_x, u_y, v_x, v_y)[:, None]


def solution(mesh):
    return jax.shard_map(
        per_device,
        mesh=mesh,
        in_specs=(
            P(None, "grp", "gx", "gy", None),
            P(None, "grp", "gx", "gy", None),
            P("grp", "gx", "gy", None, None, None),
            P(None, "grp", "gx", "gy", None, None, None),
            P("grp", "gx", "gy", None, None, None),
        ),
        out_specs=P(None, "grp", "gx", "gy", None),
        check_vma=False,
    )
```

time: 54.8 us -> 38.4 us (0.70); the launches traced: 53.7 us -> 38.2 us
  Pallas kernels: 53.7 us -> 38.2 us
    pallas_call x3 -> x1, Pallas kernels: 51.2 us -> 35.7 us  [section(): pl.pallas_call(section_kernel, out_shape=(jax.ShapeDtypeStruct((8, 8, 16,...]
where the time goes in v2:
time: 38.4 us; the launch traced here: 38.2 us
  Pallas kernels  38.2 us (99%)
    pallas_call x1, Pallas kernels, section(): pl.pallas_call(section_kernel, out_shape=(jax.ShapeDtypeStruct((8, 8, 16,...  35.7 us
    pallas_call x1, Pallas kernels, step(): pl.pallas_call(step_kernel, out_shape=jax.ShapeDtypeStruct((8, 8, 16, 128...  2.56 us

profile of v2, /device:TPU:1, one launch (start us, length us, event | category | flops | bytes accessed | tf_op | source)
XLA Modules:
  0.0 38.2 jit_solution(3080696453398895020)
XLA Ops:
  0.0 35.7 %section.1 = (f32[8,8,16,128]{3,2,1,0:T(8,128)}, f32[2,8,16,128]{3,2,1,0:T(8,128)}, f32[2,8,8,128]{3,2,1,0:T(8,128)}, f32[2,3,16,128]{3,2,1,0:T(8,128)}, f32[2,3,8,128]{3,2,1,0:T(8,128)}) custom-call(f32[8,8,16,128]{3,2,1,0:T(8,128)} %bitcast.16, f32[3,8,16,128]{3,2,1,0:T(8,128)} %bitcast.14, s32[4,32,64]{2,1,0:T(8,128)} %bitcast.18, ...), custom_call_target="tpu_custom_call" | custom-call | tf_op jit(solution)/shard_map/section/pallas_call | solution.py:255
  35.7 2.6 %step.1 = f32[8,8,16,128]{3,2,1,0:T(8,128)} custom-call(f32[8,8,16,128]{3,2,1,0:T(8,128)} %get-tuple-element.10.u_ref, f32[3,8,16,128]{3,2,1,0:T(8,128)} %bitcast.15, f32[2,8,16,128]{3,2,1,0:T(8,128)} %get-tuple-element.11.ux_ref, f32[2,8,8,128]{3,2,1,0:T(8,128)} %get-tuple-element.12.uy_ref, f32[2,3,16,128]{3,2,1,0:T(8,128)} %get-tuple-element.13.vx_ref, ...), custom_call_target="tpu_custom_call" | custom-call | tf_op jit(solution)/shard_map/step/pallas_call | solution.py:392

commit v3 on v2

--- a/solution.py
+++ b/solution.py
@@ -23,7 +23,7 @@
 
 
 def packed_rows(block):
-    return jnp.concatenate([block[0:8], block[16:24], block[8:16], block[24:32]], axis=1)
+    return jnp.concatenate([block[8 * u : 8 * u + 8] for u in range(4)], axis=1)
 
 
 def neighbours():
@@ -47,6 +47,25 @@
         remote(src, dst, send.at[n], recv.at[n], where)
         for n, ((src, dst), where) in enumerate(zip(pairs, neighbours()))
     ]
+
+
+def edges():
+    i, j = lax.axis_index("gx"), lax.axis_index("gy")
+    return i < 15, i > 0, j < 3, j > 0
+
+
+def start_sides(copies):
+    for copy, there in zip(copies, edges()):
+        pl.when(there)(copy.start)
+
+
+def wait_sides(copies):
+    up_x, down_x, up_y, down_y = edges()
+    for copy, sends, comes in zip(
+        copies, (up_x, down_x, up_y, down_y), (down_x, up_x, down_y, up_y)
+    ):
+        pl.when(sends)(copy.wait_send)
+        pl.when(comes)(copy.wait_recv)
 
 
 def remote(src, dst, send, recv, where):
@@ -60,11 +79,14 @@
     )
 
 
-def interpolate(rr, lhs, ints, floats, prod, turned):
-    base = ints[pl.ds(rr, 1), :]
-    fx = floats[0, pl.ds(rr, 1), :]
-    fy = floats[1, pl.ds(rr, 1), :]
-    fz = floats[2, pl.ds(rr, 1), :]
+def interpolate(n, t, lhs, ints, floats, prod, turned):
+    def two(ref):
+        return jnp.concatenate(
+            [ref[pl.ds(n * 8 + 2 * t, 1), :], ref[pl.ds(n * 8 + 2 * t + 1, 1), :]], axis=1
+        )
+
+    base = two(ints)
+    fx, fy, fz = (two(floats.at[d]) for d in range(3))
     cz = base & 127
     cy = (base >> 7) & 15
     cx = base >> 11
@@ -86,8 +108,9 @@
             total = total + prod[start : start + 16, :] * wx[x]
         rows.append(jnp.sum(total * wy, axis=0, keepdims=True))
     values = jnp.concatenate(rows, axis=0)
-    turned[pl.ds(pl.multiple_of(rr * 8, 8), 8), :] = values[:, 0:128]
-    turned[pl.ds(pl.multiple_of(64 + rr * 8, 8), 8), :] = values[:, 128:256]
+    turned[pl.ds(pl.multiple_of(t * 16, 16), 16), :] = jnp.concatenate(
+        [values[:, 0:128], values[:, 128:256]], axis=0
+    )
 
 
 def spots(ints, rr):
@@ -98,13 +121,27 @@
 
 
 def section_kernel(
-    state_ref, vel_ref, corner_ref, frac_ref, target_ref,
+    state_in, vel_in, corner_in, frac_in, target_in,
     filled, u_x, u_y, v_x, v_y,
-    lhs, ints, floats, prods, turned, first, second, third, put_rows, put_lanes, acc, cells,
-    face_u, face_v,
+    lhs, ints, floats, prods, turned, first, second, third, fourth, put_rows, put_lanes, acc, cells,
+    face_u, face_v, state_ref, vel_ref, corner_ref, frac_ref, target_ref, loads,
     y_send, y_recv, d_send, d_recv, v_send, v_recv, u_send, u_recv,
 ):
     g, i, j = lax.axis_index("grp"), lax.axis_index("gx"), lax.axis_index("gy")
+    state_load, corner_load, frac_load, vel_load, target_load = (
+        pltpu.make_async_copy(src, dst, loads.at[n])
+        for n, (src, dst) in enumerate(
+            (
+                (state_in, state_ref),
+                (corner_in, corner_ref),
+                (frac_in, frac_ref),
+                (vel_in, vel_ref),
+                (target_in, target_ref),
+            )
+        )
+    )
+    for load in (corner_load, frac_load, state_load, vel_load, target_load):
+        load.start()
     barrier = pltpu.get_barrier_semaphore()
 
     @pl.loop(0, 48)
@@ -118,61 +155,90 @@
     for where in neighbours()[:2]:
         pl.semaphore_signal(barrier, inc=1, device_id=where, device_id_type=MESH)
 
+    corner_load.wait()
+    frac_load.wait()
+    for k in range(3):
+        h = lax.rem(g + grid_step(k), 4)
+        for c in range(2):
+            at = slice((3 * c + k) * 8, (3 * c + k) * 8 + 8)
+            here = slice(32 * c, 32 * c + 32)
+            ints[at, :] = packed_rows(corner_ref[h, :, here])
+            for d in range(3):
+                floats[d, at, :] = packed_rows(frac_ref[d, h, :, here])
+
+    state_load.wait()
     head, rest = halves(state_ref[...].reshape(1024, 128))
     lhs[:, 0:128] = head
     lhs[:, 128:256] = rest
+    vel_load.wait()
     face_v[0] = vel_ref[:, :, 0, :]
     face_v[1] = vel_ref[:, :, 15, :]
     v_sides = side_copies(vel_ref, face_v, v_x, v_y, v_send, v_recv)
 
-    def onward(k):
-        some = first.at[0, :, :, 0:3]
-        remote(some, second.at[k, :, :, 0:3], y_send, y_recv.at[k], {"gx": i}).wait_recv()
-
-        @pl.loop(0, 16)
+    def onward(n):
+        remote(first.at[n, 0:3], second.at[n, 0:3], y_send, y_recv.at[n], {"gx": i}).wait_recv()
+        for came in range(4):
+            for u in range(2):
+                third[pl.ds(n * 64 + u * 4 + came, 8, stride=8), :] = second[
+                    n, came, u * 8 : u * 8 + 8
+                ]
+        c, k = n // 3, lax.rem(n, 3)
+
+        @pl.loop(0, 8)
         def _(to):
-            where = {"grp": lax.rem(g + grid_step(k), 4), "gx": to}
-            remote(second.at[k, :, to], third.at[k, :, i], d_send, d_recv.at[k], where).start()
-
-    @pl.loop(0, 3)
-    def _(k):
-        h = lax.rem(g + grid_step(k), 4)
-        ints[...] = packed_rows(corner_ref[h])
-        for d in range(3):
-            floats[d] = packed_rows(frac_ref[d, h])
-
-        @pl.loop(0, 8 // len(prods))
+            where = {"grp": lax.rem(g + grid_step(k), 4), "gx": c * 8 + to}
+            remote(
+                third.at[pl.ds(pl.multiple_of(n * 64 + to * 8, 8), 8)],
+                fourth.at[pl.ds(pl.multiple_of(k * 128 + i * 8, 8), 8)],
+                d_send,
+                d_recv.at[k],
+                where,
+            ).start()
+
+    early = (15 - i) // 8
+    wait_at = 5 * early
+
+    @pl.loop(0, 6)
+    def _(n):
+        @pl.loop(0, 4 // len(prods))
         def _(step):
-            for n, prod in enumerate(prods):
-                interpolate(step * len(prods) + n, lhs, ints, floats, prod, turned)
-
-        first[k] = turned[...].T.reshape(2, 16, 4, 1, 128)
-        second[k, :, :, j] = first[k, :, :, j]
-
-        @pl.when(k == 0)
+            for m, prod in enumerate(prods):
+                interpolate(n, step * len(prods) + m, lhs, ints, floats, prod, turned)
+
+        both = jnp.concatenate([turned[0:64, 0:64], turned[0:64, 64:128]], axis=0)
+        turned[0:64, :] = both.T
+        for to in range(4):
+            first[n, to] = turned[pl.ds(to, 16, stride=4), :]
+        second[n, j] = first[n, j]
+
+        @pl.when(n == wait_at)
         def _():
             pl.semaphore_wait(barrier, 53)
-
-        for d in range(1, 4):
-            to = lax.rem(j + d, 4)
-            remote(
-                first.at[k, :, :, to], second.at[k, :, :, j], y_send, y_recv.at[k], {"gy": to}
-            ).start()
-
-        @pl.when(k == 0)
+            start_sides(v_sides)
+
+        @pl.when(n >= wait_at)
         def _():
-            for copy in v_sides:
-                copy.start()
-
-        @pl.when(k > 0)
+            @pl.loop(lax.rem(n, 5) * (1 - early) + 5 * (n // 5) * (1 - early), n + 1)
+            def _(m):
+                for d in range(1, 4):
+                    to = lax.rem(j + d, 4)
+                    remote(
+                        first.at[m, to], second.at[m, j], y_send, y_recv.at[m], {"gy": to}
+                    ).start()
+
+        @pl.when(n >= wait_at + 2)
         def _():
-            onward(k - 1)
+            onward(n - 2)
+
+    target_load.wait()
 
     @pl.loop(0, 3)
     def _(k):
         cells[k] = packed_rows(target_ref[lax.rem(g + 4 - grid_step(k), 4)])
 
-    onward(2)
+    @pl.loop(4 * (1 - early), 6)
+    def _(n):
+        onward(n)
 
     @pl.loop(0, 24)
     def _(n):
@@ -187,38 +253,40 @@
 
     @pl.loop(0, 3)
     def _(k):
-        remote(second.at[k], third.at[k], d_send, d_recv.at[k], {"gx": i}).wait_recv()
-        turned[...] = third[k].reshape(128, 128).T
-
-        @pl.loop(0, 8)
-        def _(rr):
-            row, _ = spots(cells.at[k], rr)
-            values = jnp.concatenate(
-                [
-                    turned[pl.ds(pl.multiple_of(rr * 8, 8), 8), :],
-                    turned[pl.ds(pl.multiple_of(64 + rr * 8, 8), 8), :],
-                ],
-                axis=1,
+        mine = pl.ds(pl.multiple_of(k * 128, 128), 128)
+        remote(third.at[mine], fourth.at[mine], d_send, d_recv.at[k], {"gx": i}).wait_recv()
+        for u in range(2):
+            for came in range(4):
+                turned[pl.ds(u * 64 + came, 16, stride=4), :] = fourth[
+                    pl.ds(k * 128 + u * 4 + came, 16, stride=8), :
+                ]
+        turned[...] = turned[...].T
+        for part, put in enumerate(put_rows):
+            for m in range(8 // len(put_rows)):
+                r = part * (8 // len(put_rows)) + m
+                row, _ = spots(cells.at[k], r)
+                values = jnp.concatenate(
+                    [turned[r * 8 : r * 8 + 8, :], turned[64 + r * 8 : 72 + r * 8, :]], axis=1
+                )
+                head = values.astype(bf16).astype(f32)
+                rest = values - head
+                hit = lax.broadcasted_iota(jnp.int32, (32, 256), 0) == row
+                at = slice(m * 256, m * 256 + 256)
+                for v in range(8):
+                    put[v * 32 : v * 32 + 32, at] = jnp.where(hit, head[v : v + 1, :], 0.0).astype(
+                        bf16
+                    )
+                    put[256 + v * 32 : 288 + v * 32, at] = jnp.where(
+                        hit, rest[v : v + 1, :], 0.0
+                    ).astype(bf16)
+                put[512:544, at] = jnp.where(hit, 1.0, 0.0).astype(bf16)
+            span = 2048 // len(put_rows)
+            acc[...] += lax.dot_general(
+                put[...],
+                put_lanes[:, pl.ds(pl.multiple_of(k * 2048 + part * span, span), span)],
+                (((1,), (1,)), ((), ())),
+                preferred_element_type=f32,
             )
-            head = values.astype(bf16).astype(f32)
-            rest = values - head
-            hit = lax.broadcasted_iota(jnp.int32, (32, 256), 0) == row
-            at = pl.ds(pl.multiple_of(rr * 256, 256), 256)
-            for v in range(8):
-                put_rows[v * 32 : v * 32 + 32, at] = jnp.where(hit, head[v : v + 1, :], 0.0).astype(
-                    bf16
-                )
-                put_rows[256 + v * 32 : 288 + v * 32, at] = jnp.where(
-                    hit, rest[v : v + 1, :], 0.0
-                ).astype(bf16)
-            put_rows[512:544, at] = jnp.where(hit, 1.0, 0.0).astype(bf16)
-
-        acc[...] += lax.dot_general(
-            put_rows[...],
-            put_lanes[:, pl.ds(pl.multiple_of(k * 2048, 2048), 2048)],
-            (((1,), (1,)), ((), ())),
-            preferred_element_type=f32,
-        )
 
     spot = lax.broadcasted_iota(jnp.int32, (32, 128), 1)
     rim = (spot < 32) | (spot >= 96)
@@ -238,20 +306,21 @@
     face_u[0] = filled[:, :, 0, :]
     face_u[1] = filled[:, :, 15, :]
     u_sides = side_copies(filled, face_u, u_x, u_y, u_send, u_recv)
-    for copy in u_sides:
-        copy.start()
-    for copy in v_sides + u_sides:
-        copy.wait()
-    remote(first.at[:, :, :, 0:3], second.at[:, :, :, 0:3], y_send, y_recv.at[0], {"gx": i}).wait_send()
-    remote(second, third, d_send, d_recv.at[0], {"gx": i}).wait_send()
-
-
-UNROLL = 2
+    start_sides(u_sides)
+    wait_sides(v_sides)
+    wait_sides(u_sides)
+    remote(first.at[:, 0:3], second.at[:, 0:3], y_send, y_recv.at[0], {"gx": i}).wait_send()
+    remote(third, fourth, d_send, d_recv.at[0], {"gx": i}).wait_send()
+
+
+UNROLL = 4
+PARTS = 2
 
 
 def section(state, velocity, corner, frac, target):
     dma = pltpu.SemaphoreType.DMA
-    chunk = pltpu.VMEM((3, 2, 16, 4, 1, 128), f32)
+    chunk = pltpu.VMEM((6, 4, 16, 128), f32)
+    whole = pltpu.VMEM((384, 128), f32)
     return pl.pallas_call(
         section_kernel,
         out_shape=(
@@ -261,25 +330,32 @@
             jax.ShapeDtypeStruct((2, 3, 16, 128), f32),
             jax.ShapeDtypeStruct((2, 3, 8, 128), f32),
         ),
-        in_specs=[VMEM] * 5,
+        in_specs=[pl.BlockSpec(memory_space=pltpu.HBM)] * 5,
         out_specs=(VMEM,) * 5,
         scratch_shapes=[
             pltpu.VMEM((1024, 256), bf16),
-            pltpu.VMEM((8, 256), jnp.int32),
-            pltpu.VMEM((3, 8, 256), f32),
+            pltpu.VMEM((48, 128), jnp.int32),
+            pltpu.VMEM((3, 48, 128), f32),
             [pltpu.VMEM((1024, 256), f32) for _ in range(UNROLL)],
             pltpu.VMEM((128, 128), f32),
             chunk,
             chunk,
-            chunk,
-            pltpu.VMEM((544, 2048), bf16),
+            whole,
+            whole,
+            [pltpu.VMEM((544, 2048 // PARTS), bf16) for _ in range(PARTS)],
             pltpu.VMEM((256, 6144), bf16),
             pltpu.VMEM((544, 256), f32),
             pltpu.VMEM((3, 8, 256), jnp.int32),
             pltpu.VMEM((2, 8, 8, 128), f32),
             pltpu.VMEM((2, 3, 8, 128), f32),
+            pltpu.VMEM((8, 8, 16, 128), f32),
+            pltpu.VMEM((3, 8, 16, 128), f32),
+            pltpu.VMEM((4, 32, 64), jnp.int32),
+            pltpu.VMEM((3, 4, 32, 64), f32),
+            pltpu.VMEM((4, 32, 64), jnp.int32),
+            dma((5,)),
             dma,
-            dma((3,)),
+            dma((6,)),
             dma,
             dma((3,)),
             dma((4,)),
@@ -287,7 +363,9 @@
             dma((4,)),
             dma((4,)),
         ],
-        compiler_params=pltpu.CompilerParams(collective_id=0, has_side_effects=True),
+        compiler_params=pltpu.CompilerParams(
+            collective_id=0, has_side_effects=True, vmem_limit_bytes=24 << 20
+        ),
         name="section",
     )(state, velocity, corner, frac, target)
 
@@ -394,6 +472,7 @@
         out_shape=jax.ShapeDtypeStruct((8, 8, 16, 128), f32),
         in_specs=[VMEM] * 6,
         out_specs=VMEM,
+        compiler_params=pltpu.CompilerParams(vmem_limit_bytes=8 << 20),
         name="step",
     )(u, vel, ux, uy, vx, vy)
 
@@ -404,7 +483,10 @@
     corner = donor_corner[0, 0, 0].transpose(0, 2, 1)
     frac = donor_fraction[:, 0, 0, 0].transpose(0, 1, 3, 2)
     target = target_cell[0, 0, 0].transpose(0, 2, 1)
-    filled, u_x, u_y, v_x, v_y = section(state, speeds, corner, frac, target)
+    state, far_speeds, corner, frac, target = (
+        pltpu.with_memory_space_constraint(x, pltpu.HBM) for x in (state, speeds, corner, frac, target)
+    )
+    filled, u_x, u_y, v_x, v_y = section(state, far_speeds, corner, frac, target)
     return step(filled, speeds, u_x, u_y, v_x, v_y)[:, None]
 
 

time: 38.4 us -> 32.3 us (0.84)
  Pallas kernels: 38.2 us -> 32.2 us
    pallas_call x1, Pallas kernels: 35.7 us -> 30.8 us  [section(): pl.pallas_call(section_kernel, out_shape=(jax.ShapeDtypeStruct((8, 8, 16,...]
    pallas_call x1, Pallas kernels: 2.56 us -> 1.37 us  [step(): pl.pallas_call(step_kernel, out_shape=jax.ShapeDtypeStruct((8, 8, 16, 128...]
where the time goes in v3:
time: 32.3 us; the launch traced here: 32.2 us
  Pallas kernels  32.2 us (100%)
    pallas_call x1, Pallas kernels, section(): pl.pallas_call(section_kernel, out_shape=(jax.ShapeDtypeStruct((8, 8, 16,...  30.8 us
    pallas_call x1, Pallas kernels, step(): pl.pallas_call(step_kernel, out_shape=jax.ShapeDtypeStruct((8, 8, 16, 128...  1.37 us

profile of v3, /device:TPU:1, one launch (start us, length us, event | category | flops | bytes accessed | tf_op | source)
XLA Modules:
  0.0 32.2 jit_solution(2311019681429441114)
XLA Ops:
  0.0 0.0 copy-start
  0.0 30.8 %section.1 = (f32[8,8,16,128]{3,2,1,0:T(8,128)S(1)}, f32[2,8,16,128]{3,2,1,0:T(8,128)S(1)}, f32[2,8,8,128]{3,2,1,0:T(8,128)S(1)}, f32[2,3,16,128]{3,2,1,0:T(8,128)S(1)}, f32[2,3,8,128]{3,2,1,0:T(8,128)S(1)}) custom-call(f32[8,8,16,128]{3,2,1,0:T(8,128)} %bitcast.16, f32[3,8,16,128]{3,2,1,0:T(8,128)} %bitcast.14, s32[4,32,64]{2,1,0:T(8,128)} %bitcast.18, ...), custom_call_target="tpu_custom_call" | custom-call | tf_op jit(solution)/shard_map/section/pallas_call | solution.py:324
  30.8 0.0 copy-done
  30.8 1.4 %step.1 = f32[8,8,16,128]{3,2,1,0:T(8,128)} custom-call(f32[8,8,16,128]{3,2,1,0:T(8,128)S(1)} %get-tuple-element.10.u_ref, f32[3,8,16,128]{3,2,1,0:T(8,128)S(1)} %bitcast.15, f32[2,8,16,128]{3,2,1,0:T(8,128)S(1)} %get-tuple-element.11.ux_ref, f32[2,8,8,128]{3,2,1,0:T(8,128)S(1)} %get-tuple-element.12.uy_ref, f32[2,3,16,128]{3,2,1,0:T(8,128)S(1)} %get-tuple-element.13.vx_ref, ...), custom_call_target="tpu_custom_call" | custom-call | tf_op jit(solution)/shard_map/step/pallas_call | solution.py:470
Async XLA Ops:
  0.0 30.8 %copy-start = (f32[3,1,8,16,128]{4,3,2,1,0:T(8,128)S(1)}, f32[3,1,8,16,128]{4,3,2,1,0:T(8,128)}, u32[]{:S(2)}) copy-start(f32[3,1,8,16,128]{4,3,2,1,0:T(8,128)} %param.6) | copy-start | bytes 589828

commit v4 on v3

--- a/solution.py
+++ b/solution.py
@@ -20,6 +20,18 @@
 
 def grid_step(k):
     return 1 + lax.rem(k + 1, 3)
+
+
+def meetings(g):
+    return 3 - g // 2
+
+
+def send_slot(g, m):
+    return m * (1 + g // 3)
+
+
+def take_slot(g, m):
+    return m * (1 + (g // 2) * (3 - g))
 
 
 def packed_rows(block):
@@ -144,10 +156,22 @@
         load.start()
     barrier = pltpu.get_barrier_semaphore()
 
-    @pl.loop(0, 48)
-    def _(n):
-        where = {"grp": lax.rem(g + 1 + n // 16, 4), "gx": lax.rem(n, 16)}
-        pl.semaphore_signal(barrier, inc=1, device_id=where, device_id_type=MESH)
+    met = meetings(g)
+
+    grids = [lax.rem(g + grid_step(send_slot(g, m)), 4) for m in range(3)]
+
+    def greet(m):
+        @pl.loop(0, 16, unroll=8)
+        def _(to):
+            where = {"grp": grids[m], "gx": to}
+            pl.semaphore_signal(barrier, inc=1, device_id=where, device_id_type=MESH)
+
+    greet(0)
+    greet(1)
+
+    @pl.when(met == 3)
+    def _():
+        greet(2)
 
     for d in range(1, 4):
         where = {"gy": lax.rem(j + d, 4)}
@@ -157,10 +181,11 @@
 
     corner_load.wait()
     frac_load.wait()
-    for k in range(3):
-        h = lax.rem(g + grid_step(k), 4)
+    @pl.loop(0, met)
+    def _(m):
+        h = lax.rem(g + grid_step(send_slot(g, m)), 4)
         for c in range(2):
-            at = slice((3 * c + k) * 8, (3 * c + k) * 8 + 8)
+            at = pl.ds(pl.multiple_of((c * met + m) * 8, 8), 8)
             here = slice(32 * c, 32 * c + 32)
             ints[at, :] = packed_rows(corner_ref[h, :, here])
             for d in range(3):
@@ -170,9 +195,6 @@
     head, rest = halves(state_ref[...].reshape(1024, 128))
     lhs[:, 0:128] = head
     lhs[:, 128:256] = rest
-    vel_load.wait()
-    face_v[0] = vel_ref[:, :, 0, :]
-    face_v[1] = vel_ref[:, :, 15, :]
     v_sides = side_copies(vel_ref, face_v, v_x, v_y, v_send, v_recv)
 
     def onward(n):
@@ -182,11 +204,14 @@
                 third[pl.ds(n * 64 + u * 4 + came, 8, stride=8), :] = second[
                     n, came, u * 8 : u * 8 + 8
                 ]
-        c, k = n // 3, lax.rem(n, 3)
-
-        @pl.loop(0, 8)
+        c = n // met
+        k = send_slot(g, n - c * met)
+
+        grid = lax.rem(g + grid_step(k), 4)
+
+        @pl.loop(0, 8, unroll=8)
         def _(to):
-            where = {"grp": lax.rem(g + grid_step(k), 4), "gx": c * 8 + to}
+            where = {"grp": grid, "gx": c * 8 + to}
             remote(
                 third.at[pl.ds(pl.multiple_of(n * 64 + to * 8, 8), 8)],
                 fourth.at[pl.ds(pl.multiple_of(k * 128 + i * 8, 8), 8)],
@@ -196,9 +221,10 @@
             ).start()
 
     early = (15 - i) // 8
-    wait_at = 5 * early
-
-    @pl.loop(0, 6)
+    chunks = 2 * met
+    wait_at = (chunks - 1) * early
+
+    @pl.loop(0, chunks)
     def _(n):
         @pl.loop(0, 4 // len(prods))
         def _(step):
@@ -213,8 +239,7 @@
 
         @pl.when(n == wait_at)
         def _():
-            pl.semaphore_wait(barrier, 53)
-            start_sides(v_sides)
+            pl.semaphore_wait(barrier, 16 * met + 5)
 
         @pl.when(n >= wait_at)
         def _():
@@ -232,15 +257,20 @@
 
     target_load.wait()
 
-    @pl.loop(0, 3)
-    def _(k):
-        cells[k] = packed_rows(target_ref[lax.rem(g + 4 - grid_step(k), 4)])
-
-    @pl.loop(4 * (1 - early), 6)
+    @pl.loop(0, met)
+    def _(m):
+        cells[m] = packed_rows(target_ref[lax.rem(g + 4 - grid_step(take_slot(g, m)), 4)])
+
+    @pl.loop((chunks - 2) * (1 - early), chunks)
     def _(n):
         onward(n)
 
-    @pl.loop(0, 24)
+    vel_load.wait()
+    face_v[0] = vel_ref[:, :, 0, :]
+    face_v[1] = vel_ref[:, :, 15, :]
+    start_sides(v_sides)
+
+    @pl.loop(0, 8 * met)
     def _(n):
         k, rr = n // 8, lax.rem(n, 8)
         _, lane = spots(cells.at[k], rr)
@@ -251,8 +281,9 @@
 
     acc[...] = jnp.zeros_like(acc)
 
-    @pl.loop(0, 3)
-    def _(k):
+    @pl.loop(0, met)
+    def _(n):
+        k = take_slot(g, n)
         mine = pl.ds(pl.multiple_of(k * 128, 128), 128)
         remote(third.at[mine], fourth.at[mine], d_send, d_recv.at[k], {"gx": i}).wait_recv()
         for u in range(2):
@@ -264,7 +295,7 @@
         for part, put in enumerate(put_rows):
             for m in range(8 // len(put_rows)):
                 r = part * (8 // len(put_rows)) + m
-                row, _ = spots(cells.at[k], r)
+                row, _ = spots(cells.at[n], r)
                 values = jnp.concatenate(
                     [turned[r * 8 : r * 8 + 8, :], turned[64 + r * 8 : 72 + r * 8, :]], axis=1
                 )
@@ -283,7 +314,7 @@
             span = 2048 // len(put_rows)
             acc[...] += lax.dot_general(
                 put[...],
-                put_lanes[:, pl.ds(pl.multiple_of(k * 2048 + part * span, span), span)],
+                put_lanes[:, pl.ds(pl.multiple_of(n * 2048 + part * span, span), span)],
                 (((1,), (1,)), ((), ())),
                 preferred_element_type=f32,
             )
@@ -309,8 +340,12 @@
     start_sides(u_sides)
     wait_sides(v_sides)
     wait_sides(u_sides)
-    remote(first.at[:, 0:3], second.at[:, 0:3], y_send, y_recv.at[0], {"gx": i}).wait_send()
-    remote(third, fourth, d_send, d_recv.at[0], {"gx": i}).wait_send()
+
+    @pl.loop(0, chunks)
+    def _(n):
+        remote(first.at[n, 0:3], second.at[n, 0:3], y_send, y_recv.at[n], {"gx": i}).wait_send()
+        mine = pl.ds(pl.multiple_of(n * 64, 64), 64)
+        remote(third.at[mine], fourth.at[mine], d_send, d_recv.at[0], {"gx": i}).wait_send()
 
 
 UNROLL = 4

time: 32.3 us -> 30 us (0.929)
  Pallas kernels: 32.2 us -> 29.9 us
    pallas_call x1, Pallas kernels: 30.8 us -> 28.5 us  [section(): pl.pallas_call(section_kernel, out_shape=(jax.ShapeDtypeStruct((8, 8, 16,...]
where the time goes in v4:
time: 30 us; the launch traced here: 29.9 us
  Pallas kernels  29.9 us (100%)
    pallas_call x1, Pallas kernels, section(): pl.pallas_call(section_kernel, out_shape=(jax.ShapeDtypeStruct((8, 8, 16,...  28.5 us
    pallas_call x1, Pallas kernels, step(): pl.pallas_call(step_kernel, out_shape=jax.ShapeDtypeStruct((8, 8, 16, 128...  1.37 us

profile of v4, /device:TPU:1, one launch (start us, length us, event | category | flops | bytes accessed | tf_op | source)
XLA Modules:
  0.0 29.9 jit_solution(4488036006341269839)
XLA Ops:
  0.0 0.0 copy-start
  0.0 28.5 %section.1 = (f32[8,8,16,128]{3,2,1,0:T(8,128)S(1)}, f32[2,8,16,128]{3,2,1,0:T(8,128)S(1)}, f32[2,8,8,128]{3,2,1,0:T(8,128)S(1)}, f32[2,3,16,128]{3,2,1,0:T(8,128)S(1)}, f32[2,3,8,128]{3,2,1,0:T(8,128)S(1)}) custom-call(f32[8,8,16,128]{3,2,1,0:T(8,128)} %bitcast.16, f32[3,8,16,128]{3,2,1,0:T(8,128)} %bitcast.14, s32[4,32,64]{2,1,0:T(8,128)} %bitcast.18, ...), custom_call_target="tpu_custom_call" | custom-call | tf_op jit(solution)/shard_map/section/pallas_call | solution.py:359
  28.5 0.0 copy-done
  28.5 1.4 %step.1 = f32[8,8,16,128]{3,2,1,0:T(8,128)} custom-call(f32[8,8,16,128]{3,2,1,0:T(8,128)S(1)} %get-tuple-element.10.u_ref, f32[3,8,16,128]{3,2,1,0:T(8,128)S(1)} %bitcast.15, f32[2,8,16,128]{3,2,1,0:T(8,128)S(1)} %get-tuple-element.11.ux_ref, f32[2,8,8,128]{3,2,1,0:T(8,128)S(1)} %get-tuple-element.12.uy_ref, f32[2,3,16,128]{3,2,1,0:T(8,128)S(1)} %get-tuple-element.13.vx_ref, ...), custom_call_target="tpu_custom_call" | custom-call | tf_op jit(solution)/shard_map/step/pallas_call | solution.py:505
Async XLA Ops:
  0.0 28.5 %copy-start = (f32[3,1,8,16,128]{4,3,2,1,0:T(8,128)S(1)}, f32[3,1,8,16,128]{4,3,2,1,0:T(8,128)}, u32[]{:S(2)}) copy-start(f32[3,1,8,16,128]{4,3,2,1,0:T(8,128)} %param.6) | copy-start | bytes 589828

commit v5 on v4

--- a/solution.py
+++ b/solution.py
@@ -137,7 +137,7 @@
     filled, u_x, u_y, v_x, v_y,
     lhs, ints, floats, prods, turned, first, second, third, fourth, put_rows, put_lanes, acc, cells,
     face_u, face_v, state_ref, vel_ref, corner_ref, frac_ref, target_ref, loads,
-    y_send, y_recv, d_send, d_recv, v_send, v_recv, u_send, u_recv,
+    ready, y_send, y_recv, d_send, d_recv, v_send, v_recv, u_send, u_recv,
 ):
     g, i, j = lax.axis_index("grp"), lax.axis_index("gx"), lax.axis_index("gy")
     state_load, corner_load, frac_load, vel_load, target_load = (
@@ -158,26 +158,41 @@
 
     met = meetings(g)
 
+    early = (15 - i) // 8
     grids = [lax.rem(g + grid_step(send_slot(g, m)), 4) for m in range(3)]
 
-    def greet(m):
-        @pl.loop(0, 16, unroll=8)
+    def greet(m, semaphore, first_to):
+        @pl.loop(0, 8, unroll=8)
         def _(to):
-            where = {"grp": grids[m], "gx": to}
-            pl.semaphore_signal(barrier, inc=1, device_id=where, device_id_type=MESH)
-
-    greet(0)
-    greet(1)
-
-    @pl.when(met == 3)
+            where = {"grp": grids[m], "gx": first_to + to}
+            pl.semaphore_signal(semaphore, inc=1, device_id=where, device_id_type=MESH)
+
+    def greet_half(semaphore, first_to):
+        greet(0, semaphore, first_to)
+        greet(1, semaphore, first_to)
+
+        @pl.when(met == 3)
+        def _():
+            greet(2, semaphore, first_to)
+
+    @pl.when(early == 1)
     def _():
-        greet(2)
-
+        greet_half(barrier, 0)
+
+    greet_half(barrier, 8)
     for d in range(1, 4):
         where = {"gy": lax.rem(j + d, 4)}
         pl.semaphore_signal(barrier, inc=1, device_id=where, device_id_type=MESH)
-    for where in neighbours()[:2]:
-        pl.semaphore_signal(barrier, inc=1, device_id=where, device_id_type=MESH)
+
+    @pl.when(i < 15)
+    def _():
+        pl.semaphore_signal(barrier, inc=1, device_id={"gx": i + 1}, device_id_type=MESH)
+
+    @pl.when(i > 0)
+    def _():
+        pl.semaphore_signal(barrier, inc=1, device_id={"gx": i - 1}, device_id_type=MESH)
+
+    greeted = 8 * met * (2 - early) + 5 - (15 - i) // 15 - i // 15
 
     corner_load.wait()
     frac_load.wait()
@@ -220,9 +235,8 @@
                 where,
             ).start()
 
-    early = (15 - i) // 8
     chunks = 2 * met
-    wait_at = (chunks - 1) * early
+    wait_at = 1 + (met - 2) * early
 
     @pl.loop(0, chunks)
     def _(n):
@@ -239,19 +253,36 @@
 
         @pl.when(n == wait_at)
         def _():
-            pl.semaphore_wait(barrier, 16 * met + 5)
-
-        @pl.when(n >= wait_at)
-        def _():
-            @pl.loop(lax.rem(n, 5) * (1 - early) + 5 * (n // 5) * (1 - early), n + 1)
-            def _(m):
-                for d in range(1, 4):
-                    to = lax.rem(j + d, 4)
-                    remote(
-                        first.at[m, to], second.at[m, j], y_send, y_recv.at[m], {"gy": to}
-                    ).start()
-
-        @pl.when(n >= wait_at + 2)
+            pl.semaphore_wait(barrier, greeted)
+
+            @pl.when(early == 0)
+            def _():
+                greet_half(ready, 0)
+
+        def along(m):
+            for d in range(1, 4):
+                to = lax.rem(j + d, 4)
+                remote(
+                    first.at[m, to], second.at[m, j], y_send, y_recv.at[m], {"gy": to}
+                ).start()
+
+        @pl.when(n == wait_at)
+        def _():
+            pl.loop(0, n + 1)(along)
+
+        @pl.when(n > wait_at)
+        def _():
+            along(n)
+
+        @pl.when(n * early == met + 1)
+        def _():
+            pl.loop(0, met)(onward)
+
+        @pl.when(n * (1 - early) == 3)
+        def _():
+            onward(0)
+
+        @pl.when(n * (1 - early) >= 3)
         def _():
             onward(n - 2)
 
@@ -261,8 +292,12 @@
     def _(m):
         cells[m] = packed_rows(target_ref[lax.rem(g + 4 - grid_step(take_slot(g, m)), 4)])
 
-    @pl.loop((chunks - 2) * (1 - early), chunks)
+    @pl.loop((chunks - 2) * (1 - early) + met * early, chunks)
     def _(n):
+        @pl.when(n == met + chunks * (1 - early))
+        def _():
+            pl.semaphore_wait(ready, 8 * met)
+
         onward(n)
 
     vel_load.wait()
@@ -389,6 +424,7 @@
             pltpu.VMEM((3, 4, 32, 64), f32),
             pltpu.VMEM((4, 32, 64), jnp.int32),
             dma((5,)),
+            pltpu.SemaphoreType.REGULAR,
             dma,
             dma((6,)),
             dma,
@@ -415,7 +451,8 @@
     )
 
 
-def step_kernel(u_ref, vel_ref, ux_ref, uy_ref, vx_ref, vy_ref, out_ref):
+def step_kernel(u_ref, vel_ref, ux_ref, uy_ref, vx_ref, vy_ref, out_hbm, out_ref, sems):
+    puts = [pltpu.make_async_copy(out_ref.at[:, x], out_hbm.at[:, x], sems.at[x]) for x in range(8)]
     i, j = lax.axis_index("gx"), lax.axis_index("gy")
     lane = lax.broadcasted_iota(jnp.int32, (16, 128), 1)
     line = lax.broadcasted_iota(jnp.int32, (16, 128), 0)
@@ -499,6 +536,9 @@
         out_ref[5, x] = u_ref[5, x] - half * (along_y(2) - along_z(1))
         out_ref[6, x] = u_ref[6, x] - half * (along_z(0) - along_x(2))
         out_ref[7, x] = u_ref[7, x] - half * (along_x(1) - along_y(0))
+        puts[x].start()
+    for put in puts:
+        put.wait()
 
 
 def step(u, vel, ux, uy, vx, vy):
@@ -506,7 +546,8 @@
         step_kernel,
         out_shape=jax.ShapeDtypeStruct((8, 8, 16, 128), f32),
         in_specs=[VMEM] * 6,
-        out_specs=VMEM,
+        out_specs=pl.BlockSpec(memory_space=pl.ANY),
+        scratch_shapes=[pltpu.VMEM((8, 8, 16, 128), f32), pltpu.SemaphoreType.DMA((8,))],
         compiler_params=pltpu.CompilerParams(vmem_limit_bytes=8 << 20),
         name="step",
     )(u, vel, ux, uy, vx, vy)

time: 30 us -> 29 us (0.967)
  Pallas kernels: 29.9 us -> 28.9 us
    pallas_call x1, Pallas kernels: 28.5 us -> 27.6 us  [section(): pl.pallas_call(section_kernel, out_shape=(jax.ShapeDtypeStruct((8, 8, 16,...]
where the time goes in v5:
time: 29 us; the launch traced here: 28.9 us
  Pallas kernels  28.9 us (100%)
    pallas_call x1, Pallas kernels, section(): pl.pallas_call(section_kernel, out_shape=(jax.ShapeDtypeStruct((8, 8, 16,...  27.6 us
    pallas_call x1, Pallas kernels, step(): pl.pallas_call(step_kernel, out_shape=jax.ShapeDtypeStruct((8, 8, 16, 128...  1.27 us

profile of v5, /device:TPU:1, one launch (start us, length us, event | category | flops | bytes accessed | tf_op | source)
XLA Modules:
  0.0 28.9 jit_solution(6737915011440703544)
XLA Ops:
  0.0 0.0 copy-start
  0.0 27.6 %section.1 = (f32[8,8,16,128]{3,2,1,0:T(8,128)S(1)}, f32[2,8,16,128]{3,2,1,0:T(8,128)S(1)}, f32[2,8,8,128]{3,2,1,0:T(8,128)S(1)}, f32[2,3,16,128]{3,2,1,0:T(8,128)S(1)}, f32[2,3,8,128]{3,2,1,0:T(8,128)S(1)}) custom-call(f32[8,8,16,128]{3,2,1,0:T(8,128)} %bitcast.16, f32[3,8,16,128]{3,2,1,0:T(8,128)} %bitcast.14, s32[4,32,64]{2,1,0:T(8,128)} %bitcast.18, ...), custom_call_target="tpu_custom_call" | custom-call | tf_op jit(solution)/shard_map/section/pallas_call | solution.py:394
  27.6 0.0 copy-done
  27.7 1.3 %step.1 = f32[8,8,16,128]{3,2,1,0:T(8,128)} custom-call(f32[8,8,16,128]{3,2,1,0:T(8,128)S(1)} %get-tuple-element.10.u_ref, f32[3,8,16,128]{3,2,1,0:T(8,128)S(1)} %bitcast.15, f32[2,8,16,128]{3,2,1,0:T(8,128)S(1)} %get-tuple-element.11.ux_ref, f32[2,8,8,128]{3,2,1,0:T(8,128)S(1)} %get-tuple-element.12.uy_ref, f32[2,3,16,128]{3,2,1,0:T(8,128)S(1)} %get-tuple-element.13.vx_ref, ...), custom_call_target="tpu_custom_call" | custom-call | tf_op jit(solution)/shard_map/step/pallas_call | solution.py:545
Async XLA Ops:
  0.0 27.7 %copy-start = (f32[3,1,8,16,128]{4,3,2,1,0:T(8,128)S(1)}, f32[3,1,8,16,128]{4,3,2,1,0:T(8,128)}, u32[]{:S(2)}) copy-start(f32[3,1,8,16,128]{4,3,2,1,0:T(8,128)} %param.6) | copy-start | bytes 589828

commit v6 on v5

--- a/solution.py
+++ b/solution.py
@@ -236,7 +236,7 @@
             ).start()
 
     chunks = 2 * met
-    wait_at = 1 + (met - 2) * early
+    wait_at = (met - 1) * early
 
     @pl.loop(0, chunks)
     def _(n):

time: 29 us -> 28.6 us (0.986)
  the two profiles are of different devices: /device:TPU:1 before, /device:TPU:99 now
where the time goes in v6:
time: 28.6 us; the launch traced here: 28.5 us
  Pallas kernels  28.5 us (100%)
    pallas_call x1, Pallas kernels, section(): pl.pallas_call(section_kernel, out_shape=(jax.ShapeDtypeStruct((8, 8, 16,...  27.3 us
    pallas_call x1, Pallas kernels, step(): pl.pallas_call(step_kernel, out_shape=jax.ShapeDtypeStruct((8, 8, 16, 128...  1.27 us

profile of v6, /device:TPU:99, one launch (start us, length us, event | category | flops | bytes accessed | tf_op | source)
XLA Modules:
  0.0 28.5 jit_solution(1110169248929411802)
XLA Ops:
  0.0 0.0 copy-start
  0.0 27.3 %section.1 = (f32[8,8,16,128]{3,2,1,0:T(8,128)S(1)}, f32[2,8,16,128]{3,2,1,0:T(8,128)S(1)}, f32[2,8,8,128]{3,2,1,0:T(8,128)S(1)}, f32[2,3,16,128]{3,2,1,0:T(8,128)S(1)}, f32[2,3,8,128]{3,2,1,0:T(8,128)S(1)}) custom-call(f32[8,8,16,128]{3,2,1,0:T(8,128)} %bitcast.16, f32[3,8,16,128]{3,2,1,0:T(8,128)} %bitcast.14, s32[4,32,64]{2,1,0:T(8,128)} %bitcast.18, ...), custom_call_target="tpu_custom_call" | custom-call | tf_op jit(solution)/shard_map/section/pallas_call | solution.py:394
  27.3 0.0 copy-done
  27.3 1.3 %step.1 = f32[8,8,16,128]{3,2,1,0:T(8,128)} custom-call(f32[8,8,16,128]{3,2,1,0:T(8,128)S(1)} %get-tuple-element.10.u_ref, f32[3,8,16,128]{3,2,1,0:T(8,128)S(1)} %bitcast.15, f32[2,8,16,128]{3,2,1,0:T(8,128)S(1)} %get-tuple-element.11.ux_ref, f32[2,8,8,128]{3,2,1,0:T(8,128)S(1)} %get-tuple-element.12.uy_ref, f32[2,3,16,128]{3,2,1,0:T(8,128)S(1)} %get-tuple-element.13.vx_ref, ...), custom_call_target="tpu_custom_call" | custom-call | tf_op jit(solution)/shard_map/step/pallas_call | solution.py:545
Async XLA Ops:
  0.0 27.3 %copy-start = (f32[3,1,8,16,128]{4,3,2,1,0:T(8,128)S(1)}, f32[3,1,8,16,128]{4,3,2,1,0:T(8,128)}, u32[]{:S(2)}) copy-start(f32[3,1,8,16,128]{4,3,2,1,0:T(8,128)} %param.6) | copy-start | bytes 589828

commit v7 on v6

--- a/solution.py
+++ b/solution.py
@@ -255,10 +255,6 @@
         def _():
             pl.semaphore_wait(barrier, greeted)
 
-            @pl.when(early == 0)
-            def _():
-                greet_half(ready, 0)
-
         def along(m):
             for d in range(1, 4):
                 to = lax.rem(j + d, 4)
@@ -270,6 +266,10 @@
         def _():
             pl.loop(0, n + 1)(along)
 
+            @pl.when(early == 0)
+            def _():
+                greet_half(ready, 0)
+
         @pl.when(n > wait_at)
         def _():
             along(n)
@@ -278,11 +278,7 @@
         def _():
             pl.loop(0, met)(onward)
 
-        @pl.when(n * (1 - early) == 3)
-        def _():
-            onward(0)
-
-        @pl.when(n * (1 - early) >= 3)
+        @pl.when(n * (1 - early) >= 2)
         def _():
             onward(n - 2)
 

time: 28.6 us -> 28.7 us (level)
  no operation moved by 1% of the time
where the time goes in v7:
time: 28.7 us; the launch traced here: 28.6 us
  Pallas kernels  28.5 us (99%)
    pallas_call x1, Pallas kernels, section(): pl.pallas_call(section_kernel, out_shape=(jax.ShapeDtypeStruct((8, 8, 16,...  27.3 us
    pallas_call x1, Pallas kernels, step(): pl.pallas_call(step_kernel, out_shape=jax.ShapeDtypeStruct((8, 8, 16, 128...  1.27 us

profile of v7, /device:TPU:99, one launch (start us, length us, event | category | flops | bytes accessed | tf_op | source)
XLA Modules:
  0.0 28.6 jit_solution(5082474870954935308)
XLA Ops:
  0.0 0.0 copy-start
  0.0 27.3 %section.1 = (f32[8,8,16,128]{3,2,1,0:T(8,128)S(1)}, f32[2,8,16,128]{3,2,1,0:T(8,128)S(1)}, f32[2,8,8,128]{3,2,1,0:T(8,128)S(1)}, f32[2,3,16,128]{3,2,1,0:T(8,128)S(1)}, f32[2,3,8,128]{3,2,1,0:T(8,128)S(1)}) custom-call(f32[8,8,16,128]{3,2,1,0:T(8,128)} %bitcast.16, f32[3,8,16,128]{3,2,1,0:T(8,128)} %bitcast.14, s32[4,32,64]{2,1,0:T(8,128)} %bitcast.18, ...), custom_call_target="tpu_custom_call" | custom-call | tf_op jit(solution)/shard_map/section/pallas_call | solution.py:390
  27.3 0.0 copy-done
  27.3 1.3 %step.1 = f32[8,8,16,128]{3,2,1,0:T(8,128)} custom-call(f32[8,8,16,128]{3,2,1,0:T(8,128)S(1)} %get-tuple-element.10.u_ref, f32[3,8,16,128]{3,2,1,0:T(8,128)S(1)} %bitcast.15, f32[2,8,16,128]{3,2,1,0:T(8,128)S(1)} %get-tuple-element.11.ux_ref, f32[2,8,8,128]{3,2,1,0:T(8,128)S(1)} %get-tuple-element.12.uy_ref, f32[2,3,16,128]{3,2,1,0:T(8,128)S(1)} %get-tuple-element.13.vx_ref, ...), custom_call_target="tpu_custom_call" | custom-call | tf_op jit(solution)/shard_map/step/pallas_call | solution.py:541
Async XLA Ops:
  0.0 27.3 %copy-start = (f32[3,1,8,16,128]{4,3,2,1,0:T(8,128)S(1)}, f32[3,1,8,16,128]{4,3,2,1,0:T(8,128)}, u32[]{:S(2)}) copy-start(f32[3,1,8,16,128]{4,3,2,1,0:T(8,128)} %param.6) | copy-start | bytes 589828
